TPU v7x, 32 devices: a whole 2x2x4 slice. The times are simulated.
32 devices in a mesh: dp: 2 (over x), col: 4 (over z), row: 4 (over y, core).
Axes of the slice: x: 2, y: 2, z: 4, core: 2. Of those that a mesh axis runs over, the one named last changes fastest.
Arguments:
- h_first: bfloat16 [64, 1024], P(('dp', 'col', 'row')), parts along dimension 0
- h_second: bfloat16 [64, 1024], P(('dp', 'col', 'row')), parts along dimension 0
- start_pos: int32 [64], P(('dp', 'col', 'row')), parts along dimension 0
- enc_lens: int32 [64], P(('dp', 'col', 'row')), parts along dimension 0
- dec_bias: float32 [32, 16], replicated
- norm_self: bfloat16 [2, 1024], replicated
- norm_cross: bfloat16 [2, 1024], replicated
- norm_mlp: bfloat16 [2, 1024], replicated
- w_query: bfloat16 [2, 1024, 1024], P(None, 'row', 'col')
- w_key: bfloat16 [2, 1024, 1024], P(None, 'row', 'col')
- w_value: bfloat16 [2, 1024, 1024], P(None, 'row', 'col')
- w_out: bfloat16 [2, 1024, 1024], P(None, 'row', 'col')
- w_cquery: bfloat16 [2, 1024, 1024], P(None, 'row', 'col')
- w_cout: bfloat16 [2, 1024, 1024], P(None, 'row', 'col')
- w_gate: bfloat16 [2, 1024, 2816], P(None, 'row', 'col')
- w_up: bfloat16 [2, 1024, 2816], P(None, 'row', 'col')
- w_down: bfloat16 [2, 2816, 1024], P(None, 'row', 'col')
- self_k: bfloat16 [2, 64, 1024, 16, 64], P(None, ('dp', 'col', 'row')), parts along dimension 1
- self_v: bfloat16 [2, 64, 1024, 16, 64], P(None, ('dp', 'col', 'row')), parts along dimension 1
- cross_k: bfloat16 [2, 64, 512, 16, 64], P(None, ('dp', 'col', 'row')), parts along dimension 1
- cross_v: bfloat16 [2, 64, 512, 16, 64], P(None, ('dp', 'col', 'row')), parts along dimension 1
Outputs:
- output 1: bfloat16 [2, 64, 1024], P(None, ('dp', 'col', 'row')), parts along dimension 1
- output 2: bfloat16 [2, 64, 1024, 16, 64], P(None, ('dp', 'col', 'row')), parts along dimension 1
- output 3: bfloat16 [2, 64, 1024, 16, 64], P(None, ('dp', 'col', 'row')), parts along dimension 1
There are 2 independent parts. A program takes and returns all parts, laid end to end along the dimension named above; an argument that names none is the same for every part.
All inputs are finite; a program needn't handle non-finite values.
Results may differ from a plain program's by a relative error of at most 0.0177046.
Values are sent between devices in bfloat16 or wider.
A program may use at most 1 GiB of HBM per device.

v0:
```python
import jax
import jax.numpy as jnp
from jax import lax
from jax.sharding import PartitionSpec as P

NORM_EPS = 1e-6
BUCKET_EDGES = (16, 19, 21, 24, 27, 31, 35, 40, 46, 52, 59, 67, 77, 87, 99, 113)


def rms_norm(hidden, gain):
    mean_sq = jnp.mean(hidden * hidden, axis=-1, keepdims=True)
    return (hidden * lax.rsqrt(mean_sq + NORM_EPS) * gain.astype(jnp.float32)).astype(jnp.bfloat16)


def project(act, weight):
    return jnp.dot(act, weight, preferred_element_type=jnp.float32).astype(jnp.bfloat16)


def attend(query_vec, keys, values, bias):
    scores = jnp.einsum('bhd,bthd->bth', query_vec, keys, preferred_element_type=jnp.float32) + bias
    attn_probs = jax.nn.softmax(scores, axis=1).astype(jnp.bfloat16)
    mixed = jnp.einsum('bth,bthd->bhd', attn_probs, values, preferred_element_type=jnp.float32)
    return mixed.astype(jnp.bfloat16).reshape(query_vec.shape[0], -1)


def position_bias(dec_bias, pos, cache_len):
    offset = pos[:, None] - jnp.arange(cache_len, dtype=jnp.int32)[None, :]
    distance = jnp.maximum(offset, 0)
    bucket_edges = jnp.array(BUCKET_EDGES, dtype=jnp.int32)
    far_bucket = BUCKET_EDGES[0] - 1 + jnp.sum((distance[:, :, None] >= bucket_edges).astype(jnp.int32), axis=-1)
    bucket = jnp.where(distance < BUCKET_EDGES[0], distance, far_bucket)
    return jnp.where((offset >= 0)[:, :, None], dec_bias[bucket], -jnp.inf)


def cross_bias(enc_lens, enc_len):
    in_range = jnp.arange(enc_len, dtype=jnp.int32)[None, :, None] < enc_lens[:, None, None]
    return jnp.where(in_range, 0.0, -jnp.inf)


def full_weight(shard):
    by_rows = lax.all_gather(shard, 'row', axis=0, tiled=True)
    return lax.all_gather(by_rows, 'col', axis=1, tiled=True)


def decode_step(hidden, pos, enc_lens, dec_bias, gains, shards, self_k, self_v, cross_k, cross_v):
    g_self, g_cross, g_mlp = gains
    w_query, w_key, w_value, w_out, w_cquery, w_cout, w_gate, w_up, w_down = shards
    num_layers, seqs, cache_len, heads, head_dim = self_k.shape
    self_mask = position_bias(dec_bias, pos, cache_len)
    cross_mask = cross_bias(enc_lens, cross_k.shape[2])
    write_mask = (jnp.arange(cache_len, dtype=jnp.int32)[None, :] == pos[:, None])[:, :, None, None]
    residual = hidden.astype(jnp.float32)
    keys_new = []
    vals_new = []
    for layer_idx in range(num_layers):
        normed = rms_norm(residual, g_self[layer_idx])
        query_vec = project(normed, full_weight(w_query[layer_idx])).reshape(seqs, heads, head_dim)
        key_row = project(normed, full_weight(w_key[layer_idx])).reshape(seqs, 1, heads, head_dim)
        val_row = project(normed, full_weight(w_value[layer_idx])).reshape(seqs, 1, heads, head_dim)
        keys_self = jnp.where(write_mask, key_row, self_k[layer_idx])
        vals_self = jnp.where(write_mask, val_row, self_v[layer_idx])
        keys_new.append(keys_self)
        vals_new.append(vals_self)
        attn_out = attend(query_vec, keys_self, vals_self, self_mask)
        residual = residual + project(attn_out, full_weight(w_out[layer_idx])).astype(jnp.float32)
        normed = rms_norm(residual, g_cross[layer_idx])
        query_vec = project(normed, full_weight(w_cquery[layer_idx])).reshape(seqs, heads, head_dim)
        attn_out = attend(query_vec, cross_k[layer_idx], cross_v[layer_idx], cross_mask)
        residual = residual + project(attn_out, full_weight(w_cout[layer_idx])).astype(jnp.float32)
        normed = rms_norm(residual, g_mlp[layer_idx])
        gate_val = project(normed, full_weight(w_gate[layer_idx]))
        up_val = project(normed, full_weight(w_up[layer_idx]))
        mlp_act = (jax.nn.silu(gate_val.astype(jnp.float32)) * up_val.astype(jnp.float32)).astype(jnp.bfloat16)
        residual = residual + project(mlp_act, full_weight(w_down[layer_idx])).astype(jnp.float32)
    return residual.astype(jnp.bfloat16), jnp.stack(keys_new), jnp.stack(vals_new)


def solution(mesh):
    batch_axes = ('dp', 'col', 'row')

    def local_step(h_first, h_second, start_pos, enc_lens, dec_bias, norm_self, norm_cross, norm_mlp,
                   w_query, w_key, w_value, w_out, w_cquery, w_cout, w_gate, w_up, w_down,
                   self_k, self_v, cross_k, cross_v):
        gains = (norm_self, norm_cross, norm_mlp)
        shards = (w_query, w_key, w_value, w_out, w_cquery, w_cout, w_gate, w_up, w_down)
        first_out, keys_one, vals_one = decode_step(h_first, start_pos, enc_lens, dec_bias, gains, shards,
                                                    self_k, self_v, cross_k, cross_v)
        second_out, keys_two, vals_two = decode_step(h_second, start_pos + 1, enc_lens, dec_bias, gains, shards,
                                                     keys_one, vals_one, cross_k, cross_v)
        return jnp.stack([first_out, second_out]), keys_two, vals_two

    row_spec = P(batch_axes, None)
    seq_spec = P(batch_axes)
    weight_spec = P(None, 'row', 'col')
    cache_spec = P(None, batch_axes)
    in_specs = (row_spec, row_spec, seq_spec, seq_spec, P(), P(), P(), P()) + (weight_spec,) * 9 + (cache_spec,) * 4
    out_specs = (P(None, batch_axes), cache_spec, cache_spec)
    return jax.shard_map(local_step, mesh=mesh, in_specs=in_specs, out_specs=out_specs, check_vma=False)
```

profile of v0, /device:TPU:0, one launch (start us, length us, event | category | flops | bytes accessed | tf_op | source)
XLA Modules:
  0.0 1391.3 jit_solution(2704722220915670123)
XLA Ops:
  15.3 10.0 all-gather.2
  25.5 9.1 all-gather
  34.7 7.2 all-gather.4
  42.0 10.5 all-gather.6
  52.6 7.2 all-gather.8
  60.0 7.2 all-gather.10
  68.6 9.0 all-gather.77.cloned.1.call-done
  77.7 7.2 all-gather.20
  84.9 10.3 all-gather.18
  95.3 7.3 all-gather.22
  102.7 7.2 all-gather.24
  110.0 10.5 all-gather.26
  120.6 7.3 all-gather.28
  129.9 5.5 gather_fusion.1
  135.5 5.6 gather_fusion
  144.5 48.7 %all-gather.63.cloned.1.call-done = bf16[1,1024,1024]{2,1,0:T(8,128)(2,1)} async-done(((bf16[1,1024,256]{2,1,0:T(8,128)(2,1)}), bf16[1,1024,1024]{2,1,0:T(8,128)(2,1)}) %all-gather.63.cloned.1.call-update) | async-done | bytes 2097168 | tf_op jit(solution)/shard_map/all_gather | solution.py:42
  195.3 45.2 %all-gather.61.cloned.1.call-done = bf16[1,1024,1024]{2,1,0:T(8,128)(2,1)} async-done(((bf16[1,1024,256]{2,1,0:T(8,128)(2,1)}), bf16[1,1024,1024]{2,1,0:T(8,128)(2,1)}) %all-gather.61.cloned.1.call-update) | async-done | bytes 2097168 | tf_op jit(solution)/shard_map/all_gather | solution.py:42
  251.1 36.7 %all-gather.65.cloned.1.call-done = bf16[1,1024,1024]{2,1,0:T(8,128)(2,1)} async-done(((bf16[1,1024,256]{2,1,0:T(8,128)(2,1)}), bf16[1,1024,1024]{2,1,0:T(8,128)(2,1)}) %all-gather.65.cloned.1.call-update) | async-done | bytes 2097168 | tf_op jit(solution)/shard_map/all_gather | solution.py:42
  292.0 3.5 fusion.44
  295.6 39.4 %all-gather.67.cloned.1.call-done = bf16[1,1024,1024]{2,1,0:T(8,128)(2,1)} async-done(((bf16[1,1024,256]{2,1,0:T(8,128)(2,1)}), bf16[1,1024,1024]{2,1,0:T(8,128)(2,1)}) %all-gather.67.cloned.1.call-update) | async-done | bytes 2097168 | tf_op jit(solution)/shard_map/all_gather | solution.py:42
  337.1 45.2 %all-gather.69.cloned.1.call-done = bf16[1,1024,1024]{2,1,0:T(8,128)(2,1)} async-done(((bf16[1,1024,256]{2,1,0:T(8,128)(2,1)}), bf16[1,1024,1024]{2,1,0:T(8,128)(2,1)}) %all-gather.69.cloned.1.call-update) | async-done | bytes 2097168 | tf_op jit(solution)/shard_map/all_gather | solution.py:42
  389.0 40.4 %all-gather.71.cloned.1.call-done = bf16[1,1024,1024]{2,1,0:T(8,128)(2,1)} async-done(((bf16[1,1024,256]{2,1,0:T(8,128)(2,1)}), bf16[1,1024,1024]{2,1,0:T(8,128)(2,1)}) %all-gather.71.cloned.1.call-update) | async-done | bytes 2097168 | tf_op jit(solution)/shard_map/all_gather | solution.py:42
  436.4 3.6 fusion.125
  448.0 87.9 %all-gather.75.cloned.1.call-done = bf16[1,1024,2816]{1,2,0:T(8,128)(2,1)} async-done(((bf16[1,1024,704]{1,2,0:T(8,128)(2,1)}), bf16[1,1024,2816]{1,2,0:T(8,128)(2,1)}) %all-gather.75.cloned.1.call-update) | async-done | bytes 5767184 | tf_op jit(solution)/shard_map/all_gather | solution.py:42
  535.8 4.4 fusion.55
  540.2 102.6 %all-gather.83.cloned.1.call-done = bf16[1,2816,1024]{2,1,0:T(8,128)(2,1)} async-done(((bf16[1,2816,256]{2,1,0:T(8,128)(2,1)}), bf16[1,2816,1024]{2,1,0:T(8,128)(2,1)}) %all-gather.83.cloned.1.call-update) | async-done | bytes 5767184 | tf_op jit(solution)/shard_map/all_gather | solution.py:42
  642.8 108.3 %all-gather.79.cloned.1.call-done = bf16[1,1024,2816]{1,2,0:T(8,128)(2,1)} async-done(((bf16[1,1024,704]{1,2,0:T(8,128)(2,1)}), bf16[1,1024,2816]{1,2,0:T(8,128)(2,1)}) %all-gather.79.cloned.1.call-update) | async-done | bytes 5767184 | tf_op jit(solution)/shard_map/all_gather | solution.py:42
  751.1 6.8 multiply_reduce_fusion.7
  757.9 4.2 fusion.61
  762.1 6.8 multiply_reduce_fusion.2
  769.0 29.3 %all-gather.87.cloned.1.call-done = bf16[1,1024,1024]{2,1,0:T(8,128)(2,1)} async-done(((bf16[1,1024,256]{2,1,0:T(8,128)(2,1)}), bf16[1,1024,1024]{2,1,0:T(8,128)(2,1)}) %all-gather.87.cloned.1.call-update) | async-done | bytes 2097168 | tf_op jit(solution)/shard_map/all_gather | solution.py:42
  800.3 45.1 %all-gather.85.cloned.1.call-done = bf16[1,1024,1024]{2,1,0:T(8,128)(2,1)} async-done(((bf16[1,1024,256]{2,1,0:T(8,128)(2,1)}), bf16[1,1024,1024]{2,1,0:T(8,128)(2,1)}) %all-gather.85.cloned.1.call-update) | async-done | bytes 2097168 | tf_op jit(solution)/shard_map/all_gather | solution.py:42
  852.9 39.7 %all-gather.89.cloned.1.call-done = bf16[1,1024,1024]{2,1,0:T(8,128)(2,1)} async-done(((bf16[1,1024,256]{2,1,0:T(8,128)(2,1)}), bf16[1,1024,1024]{2,1,0:T(8,128)(2,1)}) %all-gather.89.cloned.1.call-update) | async-done | bytes 2097168 | tf_op jit(solution)/shard_map/all_gather | solution.py:42
  899.5 3.5 fusion.40
  903.1 36.8 %all-gather.91.cloned.1.call-done = bf16[1,1024,1024]{2,1,0:T(8,128)(2,1)} async-done(((bf16[1,1024,256]{2,1,0:T(8,128)(2,1)}), bf16[1,1024,1024]{2,1,0:T(8,128)(2,1)}) %all-gather.91.cloned.1.call-update) | async-done | bytes 2097168 | tf_op jit(solution)/shard_map/all_gather | solution.py:42
  942.0 45.0 %all-gather.93.cloned.1.call-done = bf16[1,1024,1024]{2,1,0:T(8,128)(2,1)} async-done(((bf16[1,1024,256]{2,1,0:T(8,128)(2,1)}), bf16[1,1024,1024]{2,1,0:T(8,128)(2,1)}) %all-gather.93.cloned.1.call-update) | async-done | bytes 2097168 | tf_op jit(solution)/shard_map/all_gather | solution.py:42
  994.1 3.3 fusion.126
  1000.1 3.6 fusion.127
  1010.9 23.4 %all-gather.95.cloned.1.call-done = bf16[1,1024,1024]{2,1,0:T(8,128)(2,1)} async-done(((bf16[1,1024,256]{2,1,0:T(8,128)(2,1)}), bf16[1,1024,1024]{2,1,0:T(8,128)(2,1)}) %all-gather.95.cloned.1.call-update) | async-done | bytes 2097168 | tf_op jit(solution)/shard_map/all_gather | solution.py:42
  1038.5 102.1 %all-gather.99.cloned.1.call-done = bf16[1,1024,2816]{1,2,0:T(8,128)(2,1)} async-done(((bf16[1,1024,704]{1,2,0:T(8,128)(2,1)}), bf16[1,1024,2816]{1,2,0:T(8,128)(2,1)}) %all-gather.99.cloned.1.call-update) | async-done | bytes 5767184 | tf_op jit(solution)/shard_map/all_gather | solution.py:42
  1140.7 4.4 fusion.85
  1146.6 12.1 select_select_fusion.1
  1158.8 89.1 %all-gather.107.cloned.1.call-done = bf16[1,2816,1024]{2,1,0:T(8,128)(2,1)} async-done(((bf16[1,2816,256]{2,1,0:T(8,128)(2,1)}), bf16[1,2816,1024]{2,1,0:T(8,128)(2,1)}) %all-gather.107.cloned.1.call-update) | async-done | bytes 5767184 | tf_op jit(solution)/shard_map/all_gather | solution.py:42
  1247.8 108.3 %all-gather.103.cloned.1.call-done = bf16[1,1024,2816]{1,2,0:T(8,128)(2,1)} async-done(((bf16[1,1024,704]{1,2,0:T(8,128)(2,1)}), bf16[1,1024,2816]{1,2,0:T(8,128)(2,1)}) %all-gather.103.cloned.1.call-update) | async-done | bytes 5767184 | tf_op jit(solution)/shard_map/all_gather | solution.py:42
  1356.2 6.7 fusion.402
  1362.8 6.7 fusion.411
  1370.1 7.8 pad_maximum_fusion
  1377.9 6.3 pad_maximum_fusion.1
  (226 shorter events, 98.0 us)
Async XLA Ops:
  7.2 8.1 copy-start.10
  7.2 18.3 %copy-start.11 = (bf16[2,256,256]{2,1,0:T(8,128)(2,1)S(1)}, bf16[2,256,256]{2,1,0:T(8,128)(2,1)}, u32[]{:S(2)}) copy-start(bf16[2,256,256]{2,1,0:T(8,128)(2,1)} %param.32) | copy-start | bytes 786436
  7.2 60.1 %all-gather.73.cloned.1.call-start = ((), (), s32[]{:S(2)}) async-start(), calls=%async_computation.6 | async-start | bytes 1802240 | tf_op jit(solution)/shard_map/all_gather | solution.py:41
  9.3 25.4 %copy-start.12 = (bf16[2,256,256]{2,1,0:T(8,128)(2,1)S(1)}, bf16[2,256,256]{2,1,0:T(8,128)(2,1)}, u32[]{:S(2)}) copy-start(bf16[2,256,256]{2,1,0:T(8,128)(2,1)} %param.33) | copy-start | bytes 786436
  9.3 58.7 %all-gather.81.cloned.1.call-start = ((), (), s32[]{:S(2)}) async-start(), calls=%async_computation.10 | async-start | bytes 1802240 | tf_op jit(solution)/shard_map/all_gather | solution.py:41
  11.4 30.6 %copy-start.13 = (bf16[2,256,256]{2,1,0:T(8,128)(2,1)S(1)}, bf16[2,256,256]{2,1,0:T(8,128)(2,1)}, u32[]{:S(2)}) copy-start(bf16[2,256,256]{2,1,0:T(8,128)(2,1)} %param.34) | copy-start | bytes 786436
  11.4 66.2 %all-gather.77.cloned.1.call-start = ((), (), s32[]{:S(2)}) async-start(), calls=%async_computation.8 | async-start | bytes 1802240 | tf_op jit(solution)/shard_map/all_gather | solution.py:41
  13.5 39.1 %copy-start.14 = (bf16[2,256,256]{2,1,0:T(8,128)(2,1)S(1)}, bf16[2,256,256]{2,1,0:T(8,128)(2,1)}, u32[]{:S(2)}) copy-start(bf16[2,256,256]{2,1,0:T(8,128)(2,1)} %param.35) | copy-start | bytes 786436
  13.5 114.5 %all-gather.97.cloned.1.call-start = ((), (), s32[]{:S(2)}) async-start(), calls=%async_computation.18 | async-start | bytes 1802240 | tf_op jit(solution)/shard_map/all_gather | solution.py:41
  14.1 114.6 %all-gather.105.cloned.1.call-start = ((), (), s32[]{:S(2)}) async-start(), calls=%async_computation.22 | async-start | bytes 1802240 | tf_op jit(solution)/shard_map/all_gather | solution.py:41
  14.7 129.8 %all-gather.101.cloned.1.call-start = ((), (), s32[]{:S(2)}) async-start(), calls=%async_computation.20 | async-start | bytes 1802240 | tf_op jit(solution)/shard_map/all_gather | solution.py:41
  15.2 44.7 %copy-start.15 = (bf16[2,256,256]{2,1,0:T(8,128)(2,1)S(1)}, bf16[2,256,256]{2,1,0:T(8,128)(2,1)}, u32[]{:S(2)}) copy-start(bf16[2,256,256]{2,1,0:T(8,128)(2,1)} %param.36) | copy-start | bytes 786436
  15.3 178.0 %all-gather.63.cloned.1.call-start = ((), (), s32[]{:S(2)}) async-start(), calls=%async_computation.1 | async-start | bytes 2621440 | tf_op jit(solution)/shard_map/all_gather | solution.py:42
  25.4 215.1 %all-gather.61.cloned.1.call-start = ((), (), s32[]{:S(2)}) async-start(), calls=%async_computation | async-start | bytes 2621440 | tf_op jit(solution)/shard_map/all_gather | solution.py:42
  34.6 253.2 %all-gather.65.cloned.1.call-start = ((), (), s32[]{:S(2)}) async-start(), calls=%async_computation.2 | async-start | bytes 2621440 | tf_op jit(solution)/shard_map/all_gather | solution.py:42
  42.0 293.0 %all-gather.67.cloned.1.call-start = ((), (), s32[]{:S(2)}) async-start(), calls=%async_computation.3 | async-start | bytes 2621440 | tf_op jit(solution)/shard_map/all_gather | solution.py:42
  52.5 329.8 %all-gather.69.cloned.1.call-start = ((), (), s32[]{:S(2)}) async-start(), calls=%async_computation.4 | async-start | bytes 2621440 | tf_op jit(solution)/shard_map/all_gather | solution.py:42
  59.9 369.6 %all-gather.71.cloned.1.call-start = ((), (), s32[]{:S(2)}) async-start(), calls=%async_computation.5 | async-start | bytes 2621440 | tf_op jit(solution)/shard_map/all_gather | solution.py:42
  67.2 468.6 %all-gather.75.cloned.1.call-start = ((), (), s32[]{:S(2)}) async-start(), calls=%async_computation.7 | async-start | bytes 7208960 | tf_op jit(solution)/shard_map/all_gather | solution.py:42
  68.0 574.9 %all-gather.83.cloned.1.call-start = ((), (), s32[]{:S(2)}) async-start(), calls=%async_computation.11 | async-start | bytes 7208960 | tf_op jit(solution)/shard_map/all_gather | solution.py:42
  68.5 682.5 %all-gather.79.cloned.1.call-start = ((), (), s32[]{:S(2)}) async-start(), calls=%async_computation.9 | async-start | bytes 7208960 | tf_op jit(solution)/shard_map/all_gather | solution.py:42
  77.6 720.7 %all-gather.87.cloned.1.call-start = ((), (), s32[]{:S(2)}) async-start(), calls=%async_computation.13 | async-start | bytes 2621440 | tf_op jit(solution)/shard_map/all_gather | solution.py:42
  84.9 760.6 %all-gather.85.cloned.1.call-start = ((), (), s32[]{:S(2)}) async-start(), calls=%async_computation.12 | async-start | bytes 2621440 | tf_op jit(solution)/shard_map/all_gather | solution.py:42
  95.2 34.2 %copy-start.21 = (f32[32,16]{0,1:T(8,128)S(1)}, f32[32,16]{0,1:T(8,128)}, u32[]{:S(2)}) copy-start(f32[32,16]{0,1:T(8,128)} %param.27) | copy-start | bytes 6148
  95.2 34.3 %copy-start.22 = (s32[2]{0:T(128)S(1)}, s32[2]{0:T(128)}, u32[]{:S(2)}) copy-start(s32[2]{0:T(128)} %param.25) | copy-start | bytes 28
  95.2 34.4 %copy-start.23 = (s32[16]{0:T(128)S(1)}, s32[16]{0:T(128)}, u32[]{:S(2)}) copy-start(s32[16]{0:T(128)} %constant.40.clone) | copy-start | bytes 196
  95.3 797.3 %all-gather.89.cloned.1.call-start = ((), (), s32[]{:S(2)}) async-start(), calls=%async_computation.14 | async-start | bytes 2621440 | tf_op jit(solution)/shard_map/all_gather | solution.py:42
  102.7 837.2 %all-gather.91.cloned.1.call-start = ((), (), s32[]{:S(2)}) async-start(), calls=%async_computation.15 | async-start | bytes 2621440 | tf_op jit(solution)/shard_map/all_gather | solution.py:42
  110.0 877.0 %all-gather.93.cloned.1.call-start = ((), (), s32[]{:S(2)}) async-start(), calls=%async_computation.16 | async-start | bytes 2621440 | tf_op jit(solution)/shard_map/all_gather | solution.py:42
  120.6 913.7 %all-gather.95.cloned.1.call-start = ((), (), s32[]{:S(2)}) async-start(), calls=%async_computation.17 | async-start | bytes 2621440 | tf_op jit(solution)/shard_map/all_gather | solution.py:42
  127.9 1012.8 %all-gather.99.cloned.1.call-start = ((), (), s32[]{:S(2)}) async-start(), calls=%async_computation.19 | async-start | bytes 7208960 | tf_op jit(solution)/shard_map/all_gather | solution.py:42
  128.7 1119.2 %all-gather.107.cloned.1.call-start = ((), (), s32[]{:S(2)}) async-start(), calls=%async_computation.23 | async-start | bytes 7208960 | tf_op jit(solution)/shard_map/all_gather | solution.py:42
  129.4 1226.8 %all-gather.103.cloned.1.call-start = ((), (), s32[]{:S(2)}) async-start(), calls=%async_computation.21 | async-start | bytes 7208960 | tf_op jit(solution)/shard_map/all_gather | solution.py:42
  135.4 112.7 %copy-start.9 = (f32[2048,16]{1,0:T(8,128)}, f32[2048,16]{1,0:T(8,128)S(1)}, u32[]{:S(2)}) copy-start(f32[2048,16]{1,0:T(8,128)S(1)} %gather_fusion.1) | copy-start | bytes 393220
  135.4 5.7 copy-start.16
  135.4 5.9 copy-start.17
  135.4 6.0 copy-start.24
  135.5 6.2 copy-start.18
  135.5 6.2 copy-start.19
  135.5 6.3 copy-start.20
  141.1 294.2 %copy-start.8 = (f32[2048,16]{1,0:T(8,128)}, f32[2048,16]{1,0:T(8,128)S(1)}, u32[]{:S(2)}) copy-start(f32[2048,16]{1,0:T(8,128)S(1)} %gather_fusion) | copy-start | bytes 393220
  382.3 49.2 %copy-start.3 = (bf16[1,1024,1024]{2,1,0:T(8,128)(2,1)S(1)}, bf16[1,1024,1024]{2,1,0:T(8,128)(2,1)}, u32[]{:S(2)}) copy-start(bf16[1,1024,1024]{2,1,0:T(8,128)(2,1)} %all-gather.63.cloned.1.call-done) | copy-start | bytes 6291460
  440.7 6.8 copy-start.5
  892.6 6.4 copy-start.7
  903.1 90.6 %copy-start.6 = (bf16[1,1024,1024]{2,1,0:T(8,128)(2,1)S(1)}, bf16[1,1024,1024]{2,1,0:T(8,128)(2,1)}, u32[]{:S(2)}) copy-start(bf16[1,1024,1024]{2,1,0:T(8,128)(2,1)} %all-gather.87.cloned.1.call-done) | copy-start | bytes 6291460
  1000.1 3.7 copy-start.2
  1140.7 4.4 copy-start
  1370.1 7.8 copy-start.1
  (1 other events, 3.7 us)
Sparse Core Ops, SparseCore 0:
  9.5 23.5 all-gather.72
  35.3 21.8 all-gather.80
  58.7 18.8 all-gather.76
  79.0 21.6 all-gather.96
  102.7 21.4 all-gather.104
  125.6 18.8 all-gather.100
  146.0 47.1 all-gather.62
  194.8 45.6 all-gather.60
  242.1 45.6 all-gather.64
  289.3 45.6 all-gather.66
  336.6 45.6 all-gather.68
  383.7 45.6 all-gather.70
  431.0 104.7 all-gather.74
  537.2 105.5 all-gather.82
  644.2 106.8 all-gather.78
  752.5 45.7 all-gather.86
  799.7 45.6 all-gather.84
  846.8 45.6 all-gather.88
  894.1 45.6 all-gather.90
  941.3 45.6 all-gather.92
  988.6 45.6 all-gather.94
  1035.9 104.7 all-gather.98
  1142.2 105.5 all-gather.106
  1249.3 106.8 all-gather.102
where the time goes:
time: 1400 us; the launch traced here: 1390 us
  waiting for transfers between devices  1090 us (78%)
  matrix products  124 us (9%)
  blocking collectives  101 us (7%)
  other arithmetic  35.9 us (3%)
  local copies, waits for them, and re-layouts  24.5 us (2%)
  between operations  15.2 us (1%)
    all_gather x18, waiting for transfers between devices, full_weight(): return lax.all_gather(by_rows, 'col', axis=1, tiled=True)  1070 us
    all_gather x12, blocking collectives, full_weight(): by_rows = lax.all_gather(shard, 'row', axis=0, tiled=True)  101 us
    dot_general x32, matrix products, project(): jnp.dot(act, weight, preferred_element_type=jnp.float32)  81.1 us
  transfers between devices with their start and end apart: 24, of which 20 were waited for; matrix products, arithmetic and copies ran while one was open for 11% of the time, Pallas kernels for 0%

commit v1 on v0

v1 whole, which is shorter than its diff:
```python
import functools

import jax
import jax.numpy as jnp
from jax import lax
from jax.experimental import pallas as pl
from jax.experimental.pallas import tpu as pltpu
from jax.sharding import PartitionSpec as P

NORM_EPS = 1e-6
BUCKET_EDGES = (16, 19, 21, 24, 27, 31, 35, 40, 46, 52, 59, 67, 77, 87, 99, 113)
BUCKET_STARTS = tuple(range(16)) + BUCKET_EDGES
F32 = jnp.float32
BF16 = jnp.bfloat16
LAYERS = 2
SEQS = 2
TOK = 4
COLS = 4
ROWS = 4
PEERS = 16
D = 1024
HEADS = 16
T = 1024
E = 512
FB = 704
NEG = float("-inf")


def nt_dot(a, b):
    return lax.dot_general(a, b, (((1,), (1,)), ((), ())), preferred_element_type=F32)


def nn_dot(a, b):
    return jnp.dot(a, b, preferred_element_type=F32)


def body(h0_ref, h1_ref, pos_ref, len_ref, bias_ref, gs_ref, gc_ref, gm_ref,
         wq_ref, wk_ref, wv_ref, wo_ref, wcq_ref, wco_ref, wg_ref, wu_ref, wd_ref,
         sk_hbm, sv_hbm, ck_hbm, cv_hbm,
         hid_ref, krow_ref, vrow_ref,
         sk, sv, ck, cv, self_bias,
         a_send, a_recv, a_mat, p3_send, p3_recv, p1_send, p1_recv,
         gu_send, gu_recv, u_send, u_recv, u_mat,
         cache_sem, send_sem, recv_sem):
    col = lax.axis_index('col')
    row = lax.axis_index('row')
    me = col * ROWS + row

    def peer_of(k):
        other = lax.rem(me + k, PEERS)
        return other, other // ROWS, lax.rem(other, ROWS)

    cache_copies = []
    for l in range(LAYERS):
        for i, (src, dst) in enumerate(((sk_hbm, sk), (sv_hbm, sv), (ck_hbm, ck), (cv_hbm, cv))):
            cp = pltpu.make_async_copy(src.at[l], dst.at[l], cache_sem.at[l, i])
            cp.start()
            cache_copies.append(cp)

    barrier = pltpu.get_barrier_semaphore()
    for k in range(1, PEERS):
        _, c, r = peer_of(k)
        pl.semaphore_signal(barrier, inc=1, device_id={'col': c, 'row': r}, device_id_type=pl.DeviceIdType.MESH)
    pl.semaphore_wait(barrier, PEERS - 1)

    def exchange(send, recv, idx, by_row):
        for k in range(1, PEERS):
            other, c, r = peer_of(k)
            pltpu.make_async_remote_copy(
                src_ref=send.at[r if by_row else other], dst_ref=recv.at[me],
                send_sem=send_sem.at[idx], recv_sem=recv_sem.at[idx],
                device_id={'col': c, 'row': r}, device_id_type=pl.DeviceIdType.MESH).start()
        recv[me] = send[row if by_row else me]

    def arrive(recv, idx):
        part = recv.at[pl.ds(0, PEERS - 1)]
        pltpu.make_async_copy(part, part, recv_sem.at[idx]).wait()

    def left(recv, idx):
        part = recv.at[pl.ds(0, PEERS - 1)]
        pltpu.make_async_copy(part, part, send_sem.at[idx]).wait()

    jpos = lax.broadcasted_iota(jnp.int32, (HEADS, T), 1)
    for b in range(SEQS):
        p = pos_ref[b]
        for t in range(2):
            dist = p + t - jpos
            val = jnp.broadcast_to(bias_ref[:, 0:1], (HEADS, T))
            for n in range(1, 32):
                val = jnp.where(dist >= BUCKET_STARTS[n], bias_ref[:, n:n + 1], val)
            self_bias[b, pl.ds(t * HEADS, HEADS), :] = jnp.where(jpos < p, val, NEG)

    r32 = lax.broadcasted_iota(jnp.int32, (32, 8), 0)
    c8 = lax.broadcasted_iota(jnp.int32, (32, 8), 1)
    db0 = jnp.concatenate([bias_ref[:, 0:1]] * 2, axis=0)
    db1 = jnp.concatenate([bias_ref[:, 1:2]] * 2, axis=0)
    new_bias = jnp.where(c8 == 0, jnp.where(r32 < HEADS, db0, db1),
                         jnp.where((c8 == 1) & (r32 >= HEADS), db0, NEG))
    head_of = (lax.broadcasted_iota(jnp.int32, (32, D), 1) // 64) == lax.rem(
        lax.broadcasted_iota(jnp.int32, (32, D), 0), HEADS)
    jcross = lax.broadcasted_iota(jnp.int32, (32, E), 1)

    def rms(x, gain):
        mean_sq = jnp.mean(x * x, axis=-1, keepdims=True)
        return x * lax.rsqrt(mean_sq + NORM_EPS) * gain.astype(F32)

    def put_act(vec, l, e):
        for r in range(ROWS):
            a_send[l, e, r] = vec[:, r * 256:(r + 1) * 256]

    def gather_act(recv, mat):
        rows = jnp.concatenate([recv[s].astype(F32) for s in range(PEERS)], axis=0)
        return rows.astype(BF16)

    def spread_query(q4, b):
        q_first = jnp.broadcast_to(q4[b:b + 1, :], (HEADS, D))
        q_second = jnp.broadcast_to(q4[2 + b:3 + b, :], (HEADS, D))
        q = jnp.concatenate([q_first, q_second], axis=0)
        return jnp.where(head_of, q, 0.0).astype(BF16)

    def fold_heads(mixed):
        keep = jnp.where(head_of, mixed, 0.0)
        return (jnp.sum(keep[:HEADS], axis=0, keepdims=True), jnp.sum(keep[HEADS:], axis=0, keepdims=True))

    def join_tokens(pieces):
        return jnp.concatenate([pieces[0][0], pieces[1][0], pieces[0][1], pieces[1][1]], axis=0)

    def row_sum(get):
        return [(get(c * ROWS) + get(c * ROWS + 1)) + (get(c * ROWS + 2) + get(c * ROWS + 3)) for c in range(COLS)]

    def round_bf16(v):
        return v.astype(BF16).astype(F32)

    def project(vec, weight, l, e, slot):
        put_act(vec, l, e)
        exchange(a_send.at[l, e], a_recv.at[l, e], l * 12 + slot, True)
        arrive(a_recv.at[l, e], l * 12 + slot)
        prod = nn_dot(gather_act(a_recv.at[l, e], a_mat), weight)
        for s in range(PEERS):
            p1_send[l, e - 1, s] = prod[s * TOK:(s + 1) * TOK, :]
        exchange(p1_send.at[l, e - 1], p1_recv.at[l, e - 1], l * 12 + slot + 1, False)
        arrive(p1_recv.at[l, e - 1], l * 12 + slot + 1)
        sums = row_sum(lambda s: p1_recv[l, e - 1, s])
        return round_bf16(jnp.concatenate(sums, axis=1))

    x = jnp.concatenate([h0_ref[...].astype(F32), h1_ref[...].astype(F32)], axis=0)
    for l in range(LAYERS):
        base = l * 12
        n = rms(x, gs_ref[l:l + 1, :]).astype(BF16)
        put_act(n, l, 0)
        exchange(a_send.at[l, 0], a_recv.at[l, 0], base, True)
        arrive(a_recv.at[l, 0], base)
        act = gather_act(a_recv.at[l, 0], a_mat)
        for i, w in enumerate((wq_ref, wk_ref, wv_ref)):
            prod = nn_dot(act, w[l])
            for s in range(PEERS):
                p3_send[l, s, :, i * 256:(i + 1) * 256] = prod[s * TOK:(s + 1) * TOK, :]
        exchange(p3_send.at[l], p3_recv.at[l], base + 1, False)
        arrive(p3_recv.at[l], base + 1)
        sums = row_sum(lambda s: p3_recv[l, s])
        q4, k4, v4 = (round_bf16(jnp.concatenate([sm[:, i * 256:(i + 1) * 256] for sm in sums], axis=1))
                      for i in range(3))
        krow_ref[l] = k4
        vrow_ref[l] = v4
        if True:
            cache_copies[l * 4].wait()
            cache_copies[l * 4 + 1].wait()
        pieces = []
        for b in range(SEQS):
            qb = spread_query(q4, b)
            zeros = jnp.zeros((6, D), F32)
            kn = jnp.concatenate([k4[b:b + 1], k4[2 + b:3 + b], zeros], axis=0).astype(BF16)
            vn = jnp.concatenate([v4[b:b + 1], v4[2 + b:3 + b], zeros], axis=0).astype(BF16)
            old = nn_dot(qb, sk[l, b]) + self_bias[b]
            new = nt_dot(qb, kn) + new_bias
            top = jnp.maximum(jnp.max(old, axis=1, keepdims=True), jnp.max(new, axis=1, keepdims=True))
            e_old = jnp.exp(old - top)
            e_new = jnp.exp(new - top)
            total = jnp.sum(e_old, axis=1, keepdims=True) + jnp.sum(e_new, axis=1, keepdims=True)
            mixed = nt_dot((e_old / total).astype(BF16), sv[l, b]) + nn_dot((e_new / total).astype(BF16), vn)
            pieces.append(fold_heads(mixed))
        x = x + project(join_tokens(pieces).astype(BF16), wo_ref[l], l, 1, 2)

        n = rms(x, gc_ref[l:l + 1, :]).astype(BF16)
        q4 = project(n, wcq_ref[l], l, 2, 4)
        cache_copies[l * 4 + 2].wait()
        cache_copies[l * 4 + 3].wait()
        pieces = []
        for b in range(SEQS):
            qb = spread_query(q4, b)
            sc = jnp.where(jcross < len_ref[b], nn_dot(qb, ck[l, b]), NEG)
            ex = jnp.exp(sc - jnp.max(sc, axis=1, keepdims=True))
            probs = (ex / jnp.sum(ex, axis=1, keepdims=True)).astype(BF16)
            pieces.append(fold_heads(nt_dot(probs, cv[l, b])))
        x = x + project(join_tokens(pieces).astype(BF16), wco_ref[l], l, 3, 6)

        n = rms(x, gm_ref[l:l + 1, :]).astype(BF16)
        put_act(n, l, 4)
        exchange(a_send.at[l, 4], a_recv.at[l, 4], base + 8, True)
        arrive(a_recv.at[l, 4], base + 8)
        act = gather_act(a_recv.at[l, 4], a_mat)
        for i, w in enumerate((wg_ref, wu_ref)):
            prod = nt_dot(act, w[l])
            for s in range(PEERS):
                gu_send[l, s, pl.ds(i * TOK, TOK), :] = prod[s * TOK:(s + 1) * TOK, :]
        exchange(gu_send.at[l], gu_recv.at[l], base + 9, False)
        arrive(gu_recv.at[l], base + 9)
        sums = row_sum(lambda s: gu_recv[l, s])
        for c in range(COLS):
            gate = round_bf16(sums[c][:TOK])
            up = round_bf16(sums[c][TOK:])
            u_send[l, c] = (jax.nn.silu(gate) * up).astype(BF16)
        exchange(u_send.at[l], u_recv.at[l], base + 10, True)
        arrive(u_recv.at[l], base + 10)
        prod = nn_dot(gather_act(u_recv.at[l], u_mat), wd_ref[l])
        for s in range(PEERS):
            p1_send[l, 3, s] = prod[s * TOK:(s + 1) * TOK, :]
        exchange(p1_send.at[l, 3], p1_recv.at[l, 3], base + 11, False)
        arrive(p1_recv.at[l, 3], base + 11)
        sums = row_sum(lambda s: p1_recv[l, 3, s])
        x = x + round_bf16(jnp.concatenate(sums, axis=1))

    hid_ref[0] = x[0:2].astype(BF16)
    hid_ref[1] = x[2:4].astype(BF16)
    for l in range(LAYERS):
        base = l * 12
        left(a_recv.at[l, 0], base)
        left(p3_recv.at[l], base + 1)
        for e in (1, 2, 3):
            left(a_recv.at[l, e], base + 2 * e)
            left(p1_recv.at[l, e - 1], base + 2 * e + 1)
        left(a_recv.at[l, 4], base + 8)
        left(gu_recv.at[l], base + 9)
        left(u_recv.at[l], base + 10)
        left(p1_recv.at[l, 3], base + 11)


def decode(*args):
    vmem = pl.BlockSpec(memory_space=pltpu.VMEM)
    smem = pl.BlockSpec(memory_space=pltpu.SMEM)
    hbm = pl.BlockSpec(memory_space=pl.ANY)
    return pl.pallas_call(
        body,
        out_shape=(jax.ShapeDtypeStruct((2, SEQS, D), BF16),
                   jax.ShapeDtypeStruct((LAYERS, TOK, D), F32),
                   jax.ShapeDtypeStruct((LAYERS, TOK, D), F32)),
        in_specs=[vmem, vmem, smem, smem] + [vmem] * 13 + [hbm] * 4,
        out_specs=(vmem,) * 3,
        scratch_shapes=[
            pltpu.VMEM((LAYERS, SEQS, D, T), BF16),
            pltpu.VMEM((LAYERS, SEQS, D, T), BF16),
            pltpu.VMEM((LAYERS, SEQS, D, E), BF16),
            pltpu.VMEM((LAYERS, SEQS, D, E), BF16),
            pltpu.VMEM((SEQS, 32, T), F32),
            pltpu.VMEM((LAYERS, 5, ROWS, TOK, 256), BF16),
            pltpu.VMEM((LAYERS, 5, PEERS, TOK, 256), BF16),
            pltpu.VMEM((PEERS * TOK, 256), BF16),
            pltpu.VMEM((LAYERS, PEERS, TOK, 768), F32),
            pltpu.VMEM((LAYERS, PEERS, TOK, 768), F32),
            pltpu.VMEM((LAYERS, 4, PEERS, TOK, 256), F32),
            pltpu.VMEM((LAYERS, 4, PEERS, TOK, 256), F32),
            pltpu.VMEM((LAYERS, PEERS, 2 * TOK, FB), F32),
            pltpu.VMEM((LAYERS, PEERS, 2 * TOK, FB), F32),
            pltpu.VMEM((LAYERS, COLS, TOK, FB), BF16),
            pltpu.VMEM((LAYERS, PEERS, TOK, FB), BF16),
            pltpu.VMEM((PEERS * TOK, FB), BF16),
            pltpu.SemaphoreType.DMA((LAYERS, 4)),
            pltpu.SemaphoreType.DMA((LAYERS * 12,)),
            pltpu.SemaphoreType.DMA((LAYERS * 12,)),
        ],
        compiler_params=pltpu.CompilerParams(collective_id=0, has_side_effects=True,
                                             vmem_limit_bytes=60 * 1024 * 1024),
    )(*args)


def solution(mesh):
    batch_axes = ('dp', 'col', 'row')

    def local_step(h_first, h_second, start_pos, enc_lens, dec_bias, norm_self, norm_cross, norm_mlp,
                   w_query, w_key, w_value, w_out, w_cquery, w_cout, w_gate, w_up, w_down,
                   self_k, self_v, cross_k, cross_v):
        def flat(cache):
            l, b, t, h, d = cache.shape
            return cache.transpose(0, 1, 3, 4, 2).reshape(l, b, h * d, t)

        hidden, krows, vrows = decode(
            h_first, h_second, start_pos, enc_lens, dec_bias.T, norm_self, norm_cross, norm_mlp,
            w_query, w_key, w_value, w_out, w_cquery, w_cout,
            w_gate.transpose(0, 2, 1), w_up.transpose(0, 2, 1), w_down,
            flat(self_k), flat(self_v), flat(cross_k), flat(cross_v))

        at = jnp.arange(T, dtype=jnp.int32)[None, None, :, None, None]
        first = at == start_pos[None, :, None, None, None]
        second = at == (start_pos + 1)[None, :, None, None, None]

        def write(cache, rows):
            rows = rows.astype(BF16).reshape(LAYERS, 2, SEQS, 1, HEADS, 64)
            return jnp.where(first, rows[:, 0], jnp.where(second, rows[:, 1], cache))

        return hidden, write(self_k, krows), write(self_v, vrows)

    row_spec = P(batch_axes, None)
    seq_spec = P(batch_axes)
    weight_spec = P(None, 'row', 'col')
    cache_spec = P(None, batch_axes)
    in_specs = (row_spec, row_spec, seq_spec, seq_spec, P(), P(), P(), P()) + (weight_spec,) * 9 + (cache_spec,) * 4
    out_specs = (P(None, batch_axes), cache_spec, cache_spec)
    return jax.shard_map(local_step, mesh=mesh, in_specs=in_specs, out_specs=out_specs, check_vma=False)
```

time: 1400 us -> 160 us (0.11)
  waiting for transfers between devices: 1090 us -> 0 us
  Pallas kernels: 0 us -> 143 us
  matrix products: 124 us -> 0 us
  blocking collectives: 101 us -> 0 us
  local copies, waits for them, and re-layouts: 24.5 us -> 0.8 us
  other arithmetic: 35.9 us -> 15 us
  between operations: 15.2 us -> 0.65 us
    all_gather x24 -> x0, waiting for transfers between devices: 1080 us -> none  [the longest x18 1070 us: full_weight(): return lax.all_gather(by_rows, 'col', axis=1, tiled=True)]
    pallas_call x0 -> x1, Pallas kernels: none -> 143 us  [decode(): pl.pallas_call(body, out_shape=(jax.ShapeDtypeStruct((2, SEQS, D), BF16),...]
    dot_general x48 -> x0, matrix products: 124 us -> none  [the longest x32 81.1 us: project(): jnp.dot(act, weight, preferred_element_type=jnp.float32)]
    all_gather x12 -> x0, blocking collectives: 101 us -> none  [full_weight(): by_rows = lax.all_gather(shard, 'row', axis=0, tiled=True)]
    another operation x3 -> x0, other arithmetic: 14.7 us -> none  [the longest x1 7.76 us: decode_step(): jnp.stack(keys_new)]
  transfers between devices with their start and end apart: 24 -> 0, of which waited for: 20 -> 0; matrix products, arithmetic and copies ran while one was open for 11% -> 0% of each run, Pallas kernels for 0% -> 0%
where the time goes in v1:
time: 160 us; the launch traced here: 159 us
  Pallas kernels  143 us (89%)
  other arithmetic  15 us (9%)
    pallas_call x1, Pallas kernels, decode(): pl.pallas_call(body, out_shape=(jax.ShapeDtypeStruct((2, SEQS, D), BF16),...  143 us
    select_n x1, other arithmetic, write(): return jnp.where(first, rows[:, 0], jnp.where(second, rows[:, 1], cache))  12 us

profile of v1, /device:TPU:0, one launch (start us, length us, event | category | flops | bytes accessed | tf_op | source)
XLA Modules:
  0.0 159.4 jit_solution(1803870531294248803)
XLA Ops:
  0.6 0.7 broadcast_add_fusion
  1.3 0.7 iota_compare_fusion
  2.0 143.0 %shard_map.220 = (bf16[2,2,1024]{2,1,0:T(2,128)(2,1)}, f32[2,4,1024]{2,1,0:T(4,128)}, f32[2,4,1024]{2,1,0:T(4,128)}) custom-call(bf16[2,1024]{1,0:T(2,128)(2,1)} %h0_ref.1, bf16[2,1024]{1,0:T(2,128)(2,1)} %h1_ref.1, s32[2]{0:T(128)} %pos_ref.1, s32[2]{0:T(128)} %len_ref.1, f32[16,32]{1,0:T(8,128)} %bitcast.29, bf16[2,1024]{1,0:T(2,128)(2,1)} %gs_ref.1, ...), custom_call_target="tpu_custom_call" | custom-call | tf_op jit(solution)/shard_map/pallas_call | solution.py:242
  145.0 0.8 convert_element_type.6
  145.8 0.1 reshape.82
  145.9 0.8 convert_element_type.7
  146.7 0.1 reshape.83
  146.8 0.0 copy-start
  146.8 12.0 %select_select_fusion = (bf16[2,2,1024,16,64]{2,4,3,1,0:T(8,128)(2,1)}, bf16[2,2,1024,16,64]{2,4,3,1,0:T(8,128)(2,1)}) fusion(bf16[2,2,1024,16,64]{2,4,3,1,0:T(8,128)(2,1)} %param.39, pred[2,1024]{1,0:T(4,128)(4,1)S(1)} %get-tuple-element.17, pred[2,1024]{1,0:T(4,128)(4,1)S(1)} %get-tuple-element.18, bf16[2,2,16,64]{3,2,1,0:T(8,128)(2,1)S(1)} %get-tuple-element.10, ...), kind=kLoop, calls=%fused_computation | loop fusion | flops 16777216 | bytes 33591296 | tf_op jit(solution)/shard_map/jit(_where)/select_n | solution.py:298
  158.8 0.0 copy-done
  158.8 0.6 copy.25
  (1 shorter events, 0.0 us)
Async XLA Ops:
  146.8 12.0 %copy-start = (bf16[2,2,1024]{2,1,0:T(2,128)(2,1)S(1)}, bf16[2,2,1024]{2,1,0:T(2,128)(2,1)}, u32[]{:S(2)}) copy-start(bf16[2,2,1024]{2,1,0:T(2,128)(2,1)} %get-tuple-element.22) | copy-start | bytes 24580

commit v2 on v1

v2 whole, which is shorter than its diff:
```python
import functools

import jax
import jax.numpy as jnp
from jax import lax
from jax.experimental import pallas as pl
from jax.experimental.pallas import tpu as pltpu
from jax.sharding import PartitionSpec as P

NORM_EPS = 1e-6
BUCKET_EDGES = (16, 19, 21, 24, 27, 31, 35, 40, 46, 52, 59, 67, 77, 87, 99, 113)
BUCKET_STARTS = tuple(range(16)) + BUCKET_EDGES
F32 = jnp.float32
BF16 = jnp.bfloat16
LAYERS = 2
SEQS = 2
TOK = 4
COLS = 4
ROWS = 4
PEERS = 16
D = 1024
HEADS = 16
T = 1024
E = 512
FB = 704
FS = 176
NEG = float("-inf")


def nt_dot(a, b):
    return lax.dot_general(a, b, (((1,), (1,)), ((), ())), preferred_element_type=F32)


def nn_dot(a, b):
    return jnp.dot(a, b, preferred_element_type=F32)


def body(h0_ref, h1_ref, pos_ref, len_ref, bias_ref, gs_ref, gc_ref, gm_ref,
         wq_hbm, wk_hbm, wv_hbm, wo_hbm, wcq_hbm, wco_hbm, wg_hbm, wu_hbm, wd_hbm,
         sk_hbm, sv_hbm, ck_hbm, cv_hbm,
         hid_ref, new_ref,
         sk, sv, ck, cv, self_bias, proj_w, gate_w, up_w, down_w,
         a_send, a_recv, p3_send, p3_recv, p1_send, p1_recv,
         n_send, n_recv, d_send, d_recv,
         cache_sem, weight_sem, mlp_send_sem, mlp_recv_sem, send_sem, recv_sem):
    col = lax.axis_index('col')
    row = lax.axis_index('row')
    me = col * ROWS + row

    def peer_of(k):
        other = lax.rem(me + k, PEERS)
        return other, other // ROWS, lax.rem(other, ROWS)

    weight_copies = []
    for i, src in enumerate((wq_hbm, wk_hbm, wv_hbm, wo_hbm, wcq_hbm, wco_hbm)):
        cp = pltpu.make_async_copy(src, proj_w.at[i], weight_sem.at[i])
        cp.start()
        weight_copies.append(cp)
    cache_copies = []
    for l in range(LAYERS):
        for i, (src, dst) in enumerate(((sk_hbm, sk), (sv_hbm, sv), (ck_hbm, ck), (cv_hbm, cv))):
            cp = pltpu.make_async_copy(src.at[l], dst.at[l], cache_sem.at[l, i])
            cp.start()
            cache_copies.append(cp)

    barrier = pltpu.get_barrier_semaphore()
    for k in range(1, PEERS):
        _, c, r = peer_of(k)
        pl.semaphore_signal(barrier, inc=1, device_id={'col': c, 'row': r}, device_id_type=pl.DeviceIdType.MESH)
    pl.semaphore_wait(barrier, PEERS - 1)

    def exchange(send, recv, idx, by_row):
        def pick(r, other):
            return 0 if by_row is None else (r if by_row else other)

        for k in range(1, PEERS):
            other, c, r = peer_of(k)
            pltpu.make_async_remote_copy(
                src_ref=send.at[pick(r, other)], dst_ref=recv.at[me],
                send_sem=send_sem.at[idx], recv_sem=recv_sem.at[idx],
                device_id={'col': c, 'row': r}, device_id_type=pl.DeviceIdType.MESH).start()
        recv[me] = send[pick(row, me)]

    def arrive(recv, idx):
        part = recv.at[pl.ds(0, PEERS - 1)]
        pltpu.make_async_copy(part, part, recv_sem.at[idx]).wait()

    def left(recv, idx):
        part = recv.at[pl.ds(0, PEERS - 1)]
        pltpu.make_async_copy(part, part, send_sem.at[idx]).wait()

    def build_bias():
        jpos = lax.broadcasted_iota(jnp.int32, (HEADS, T), 1)
        for b in range(SEQS):
            p = pos_ref[b]
            for t in range(2):
                dist = p + t - jpos
                val = jnp.broadcast_to(bias_ref[:, 0:1], (HEADS, T))
                for n in range(1, 32):
                    val = jnp.where(dist >= BUCKET_STARTS[n], bias_ref[:, n:n + 1], val)
                self_bias[b, pl.ds(t * HEADS, HEADS), :] = jnp.where(jpos < p, val, NEG)

    r32 = lax.broadcasted_iota(jnp.int32, (32, 8), 0)
    c8 = lax.broadcasted_iota(jnp.int32, (32, 8), 1)
    db0 = jnp.concatenate([bias_ref[:, 0:1]] * 2, axis=0)
    db1 = jnp.concatenate([bias_ref[:, 1:2]] * 2, axis=0)
    new_bias = jnp.where(c8 == 0, jnp.where(r32 < HEADS, db0, db1),
                         jnp.where((c8 == 1) & (r32 >= HEADS), db0, NEG))
    head_of = (lax.broadcasted_iota(jnp.int32, (32, D), 1) // 64) == lax.rem(
        lax.broadcasted_iota(jnp.int32, (32, D), 0), HEADS)
    jcross = lax.broadcasted_iota(jnp.int32, (32, E), 1)

    def rms(x, gain):
        mean_sq = jnp.mean(x * x, axis=-1, keepdims=True)
        return x * lax.rsqrt(mean_sq + NORM_EPS) * gain.astype(F32)

    def put_act(vec, l, e):
        for r in range(ROWS):
            a_send[l, e, r] = vec[:, r * 256:(r + 1) * 256]

    def gather_act(recv):
        rows = jnp.concatenate([recv[s].astype(F32) for s in range(PEERS)], axis=0)
        return rows.astype(BF16)

    def spread_query(q4, b):
        q_first = jnp.broadcast_to(q4[b:b + 1, :], (HEADS, D))
        q_second = jnp.broadcast_to(q4[2 + b:3 + b, :], (HEADS, D))
        q = jnp.concatenate([q_first, q_second], axis=0)
        return jnp.where(head_of, q, 0.0).astype(BF16)

    def fold_heads(mixed):
        keep = jnp.where(head_of, mixed, 0.0)
        return (jnp.sum(keep[:HEADS], axis=0, keepdims=True), jnp.sum(keep[HEADS:], axis=0, keepdims=True))

    def join_tokens(pieces):
        return jnp.concatenate([pieces[0][0], pieces[1][0], pieces[0][1], pieces[1][1]], axis=0)

    def row_sum(get):
        return [(get(c * ROWS) + get(c * ROWS + 1)) + (get(c * ROWS + 2) + get(c * ROWS + 3)) for c in range(COLS)]

    def round_bf16(v):
        return v.astype(BF16).astype(F32)

    def project(vec, which, l, e, slot):
        put_act(vec, l, e)
        exchange(a_send.at[l, e], a_recv.at[l, e], l * 10 + slot, True)
        arrive(a_recv.at[l, e], l * 10 + slot)
        prod = nn_dot(gather_act(a_recv.at[l, e]), proj_w[which, l])
        for s in range(PEERS):
            p1_send[l, e - 1, s] = prod[s * TOK:(s + 1) * TOK, :]
        exchange(p1_send.at[l, e - 1], p1_recv.at[l, e - 1], l * 10 + slot + 1, False)
        arrive(p1_recv.at[l, e - 1], l * 10 + slot + 1)
        sums = row_sum(lambda s: p1_recv[l, e - 1, s])
        return round_bf16(jnp.concatenate(sums, axis=1))

    def mlp_copies(l):
        for i, (src, dst) in enumerate(((wg_hbm, gate_w), (wu_hbm, up_w))):
            for k in range(ROWS):
                r = lax.rem(row + k, ROWS)
                part = src.at[l, pl.ds(pl.multiple_of(r * FS, 16), FS), :]
                if k == 0:
                    pltpu.make_async_copy(part, dst.at[l, row], mlp_recv_sem.at[l, i]).start()
                else:
                    pltpu.make_async_remote_copy(
                        src_ref=part, dst_ref=dst.at[l, row], send_sem=mlp_send_sem.at[l, i],
                        recv_sem=mlp_recv_sem.at[l, i], device_id={'col': col, 'row': r},
                        device_id_type=pl.DeviceIdType.MESH).start()
        for k in range(ROWS):
            r = lax.rem(row + k, ROWS)
            part = wd_hbm.at[l, pl.ds(pl.multiple_of(r * FS, 16), FS), :]

            def away():
                pltpu.make_async_remote_copy(
                    src_ref=part, dst_ref=down_w.at[l, col], send_sem=mlp_send_sem.at[l, 2],
                    recv_sem=mlp_recv_sem.at[l, 2], device_id={'col': row, 'row': r},
                    device_id_type=pl.DeviceIdType.MESH).start()

            if k == 0:
                pl.when(col != row)(away)

                @pl.when(col == row)
                def _():
                    pltpu.make_async_copy(part, down_w.at[l, col], mlp_recv_sem.at[l, 2]).start()
            else:
                away()

    def mlp_arrive(l):
        for i, dst in enumerate((gate_w, up_w, down_w)):
            pltpu.make_async_copy(dst.at[l], dst.at[l], mlp_recv_sem.at[l, i]).wait()

    def mlp_left(l):
        for i, dst in enumerate((gate_w, up_w, down_w)):
            part = dst.at[l, pl.ds(0, ROWS - 1)]
            pltpu.make_async_copy(part, part, mlp_send_sem.at[l, i]).wait()

        @pl.when(col != row)
        def _():
            part = down_w.at[l, 0]
            pltpu.make_async_copy(part, part, mlp_send_sem.at[l, 2]).wait()

    x = jnp.concatenate([h0_ref[...].astype(F32), h1_ref[...].astype(F32)], axis=0)
    for l in range(LAYERS):
        base = l * 10
        n = rms(x, gs_ref[l:l + 1, :]).astype(BF16)
        put_act(n, l, 0)
        exchange(a_send.at[l, 0], a_recv.at[l, 0], base, True)
        if l == 0:
            build_bias()
            for cp in weight_copies:
                cp.wait()
        arrive(a_recv.at[l, 0], base)
        act = gather_act(a_recv.at[l, 0])
        for i in range(3):
            prod = nn_dot(act, proj_w[i, l])
            for s in range(PEERS):
                p3_send[l, s, :, i * 256:(i + 1) * 256] = prod[s * TOK:(s + 1) * TOK, :]
        exchange(p3_send.at[l], p3_recv.at[l], base + 1, False)
        mlp_copies(l)
        arrive(p3_recv.at[l], base + 1)
        sums = row_sum(lambda s: p3_recv[l, s])
        q4, k4, v4 = (round_bf16(jnp.concatenate([sm[:, i * 256:(i + 1) * 256] for sm in sums], axis=1))
                      for i in range(3))
        new_ref[pl.ds(l * 8, TOK), :] = k4
        new_ref[pl.ds(l * 8 + TOK, TOK), :] = v4
        cache_copies[l * 4].wait()
        cache_copies[l * 4 + 1].wait()
        pieces = []
        for b in range(SEQS):
            qb = spread_query(q4, b)
            zeros = jnp.zeros((6, D), F32)
            kn = jnp.concatenate([k4[b:b + 1], k4[2 + b:3 + b], zeros], axis=0).astype(BF16)
            vn = jnp.concatenate([v4[b:b + 1], v4[2 + b:3 + b], zeros], axis=0).astype(BF16)
            old = nn_dot(qb, sk[l, b]) + self_bias[b]
            new = nt_dot(qb, kn) + new_bias
            top = jnp.maximum(jnp.max(old, axis=1, keepdims=True), jnp.max(new, axis=1, keepdims=True))
            e_old = jnp.exp(old - top)
            e_new = jnp.exp(new - top)
            total = jnp.sum(e_old, axis=1, keepdims=True) + jnp.sum(e_new, axis=1, keepdims=True)
            mixed = nt_dot((e_old / total).astype(BF16), sv[l, b]) + nn_dot((e_new / total).astype(BF16), vn)
            pieces.append(fold_heads(mixed))
        x = x + project(join_tokens(pieces).astype(BF16), 3, l, 1, 2)

        n = rms(x, gc_ref[l:l + 1, :]).astype(BF16)
        q4 = project(n, 4, l, 2, 4)
        cache_copies[l * 4 + 2].wait()
        cache_copies[l * 4 + 3].wait()
        pieces = []
        for b in range(SEQS):
            qb = spread_query(q4, b)
            sc = jnp.where(jcross < len_ref[b], nn_dot(qb, ck[l, b]), NEG)
            ex = jnp.exp(sc - jnp.max(sc, axis=1, keepdims=True))
            probs = (ex / jnp.sum(ex, axis=1, keepdims=True)).astype(BF16)
            pieces.append(fold_heads(nt_dot(probs, cv[l, b])))
        x = x + project(join_tokens(pieces).astype(BF16), 5, l, 3, 6)

        n_send[l, 0] = rms(x, gm_ref[l:l + 1, :]).astype(BF16)
        exchange(n_send.at[l], n_recv.at[l], base + 8, None)
        mlp_arrive(l)
        arrive(n_recv.at[l], base + 8)
        act = gather_act(n_recv.at[l])
        gate = nt_dot(act[:, 0:256], gate_w[l, 0])
        up = nt_dot(act[:, 0:256], up_w[l, 0])
        for r in range(1, ROWS):
            gate = gate + nt_dot(act[:, r * 256:(r + 1) * 256], gate_w[l, r])
            up = up + nt_dot(act[:, r * 256:(r + 1) * 256], up_w[l, r])
        u = (jax.nn.silu(round_bf16(gate)) * round_bf16(up)).astype(BF16)
        for c in range(COLS):
            prod = nn_dot(u, down_w[l, c])
            for s in range(PEERS):
                d_send[l, s, :, c * 256:(c + 1) * 256] = prod[s * TOK:(s + 1) * TOK, :]
        exchange(d_send.at[l], d_recv.at[l], base + 9, False)
        arrive(d_recv.at[l], base + 9)
        terms = [d_recv[l, s] for s in range(PEERS)]
        while len(terms) > 1:
            terms = [terms[i] + terms[i + 1] for i in range(0, len(terms), 2)]
        x = x + round_bf16(terms[0])

    hid_ref[0] = x[0:2].astype(BF16)
    hid_ref[1] = x[2:4].astype(BF16)
    for l in range(LAYERS):
        base = l * 10
        left(a_recv.at[l, 0], base)
        left(p3_recv.at[l], base + 1)
        for e in (1, 2, 3):
            left(a_recv.at[l, e], base + 2 * e)
            left(p1_recv.at[l, e - 1], base + 2 * e + 1)
        left(n_recv.at[l], base + 8)
        left(d_recv.at[l], base + 9)
        mlp_left(l)


def write_body(pos_ref, new_ref, k_ref, v_ref, ko_ref, vo_ref, cols):
    i = pl.program_id(0)
    half = pl.program_id(1)

    @pl.when((i == 0) & (half == 0))
    def _():
        cols[...] = jnp.transpose(new_ref[...])

    b = lax.rem(i, SEQS)
    l = i // SEQS
    p = pos_ref[b]
    lanes = lax.broadcasted_iota(jnp.int32, (512, 128), 1)
    pick = lax.broadcasted_iota(jnp.int32, (512, 16), 1)
    mine = cols[pl.ds(pl.multiple_of(half * 512, 512), 512), :]
    for kv, (src, dst) in enumerate(((k_ref, ko_ref), (v_ref, vo_ref))):
        dst[...] = src[...]
        at = l * 8 + kv * TOK + b
        first = jnp.sum(jnp.where(pick == at, mine, 0.0), axis=1, keepdims=True)
        second = jnp.sum(jnp.where(pick == at + 2, mine, 0.0), axis=1, keepdims=True)
        for q in range(2):
            start = pl.multiple_of(((p + q) // 128) * 128, 128)
            old = src[0, 0, :, pl.ds(start, 128)].astype(F32)
            fresh = jnp.where(lanes + start == p, first, jnp.where(lanes + start == p + 1, second, old))
            dst[0, 0, :, pl.ds(start, 128)] = fresh.astype(BF16)


def write_caches(pos, new, k, v):
    block = pl.BlockSpec((1, 1, 512, T), lambda i, j: (i // SEQS, i % SEQS, j, 0))
    return pl.pallas_call(
        write_body,
        grid=(LAYERS * SEQS, 2),
        out_shape=(jax.ShapeDtypeStruct(k.shape, BF16),) * 2,
        in_specs=[pl.BlockSpec(memory_space=pltpu.SMEM), pl.BlockSpec((16, D), lambda i, j: (0, 0)), block, block],
        out_specs=(block, block),
        scratch_shapes=[pltpu.VMEM((D, 16), F32)],
        compiler_params=pltpu.CompilerParams(vmem_limit_bytes=14 * 1024 * 1024),
        cost_estimate=pl.CostEstimate(flops=1000000, bytes_accessed=32 << 20, transcendentals=0),
    )(pos, new, k, v)


def decode(*args):
    vmem = pl.BlockSpec(memory_space=pltpu.VMEM)
    smem = pl.BlockSpec(memory_space=pltpu.SMEM)
    hbm = pl.BlockSpec(memory_space=pltpu.HBM)
    args = tuple(pltpu.with_memory_space_constraint(a, pltpu.HBM) for a in args)
    return pl.pallas_call(
        body,
        out_shape=(jax.ShapeDtypeStruct((2, SEQS, D), BF16),
                   jax.ShapeDtypeStruct((16, D), F32)),
        in_specs=[vmem, vmem, smem, smem] + [vmem] * 4 + [hbm] * 13,
        out_specs=(vmem,) * 2,
        scratch_shapes=[
            pltpu.VMEM((LAYERS, SEQS, D, T), BF16),
            pltpu.VMEM((LAYERS, SEQS, D, T), BF16),
            pltpu.VMEM((LAYERS, SEQS, D, E), BF16),
            pltpu.VMEM((LAYERS, SEQS, D, E), BF16),
            pltpu.VMEM((SEQS, 32, T), F32),
            pltpu.VMEM((6, LAYERS, 256, 256), BF16),
            pltpu.VMEM((LAYERS, ROWS, FS, 256), BF16),
            pltpu.VMEM((LAYERS, ROWS, FS, 256), BF16),
            pltpu.VMEM((LAYERS, COLS, FS, 256), BF16),
            pltpu.VMEM((LAYERS, 4, ROWS, TOK, 256), BF16),
            pltpu.VMEM((LAYERS, 4, PEERS, TOK, 256), BF16),
            pltpu.VMEM((LAYERS, PEERS, TOK, 768), F32),
            pltpu.VMEM((LAYERS, PEERS, TOK, 768), F32),
            pltpu.VMEM((LAYERS, 3, PEERS, TOK, 256), F32),
            pltpu.VMEM((LAYERS, 3, PEERS, TOK, 256), F32),
            pltpu.VMEM((LAYERS, 1, TOK, D), BF16),
            pltpu.VMEM((LAYERS, PEERS, TOK, D), BF16),
            pltpu.VMEM((LAYERS, PEERS, TOK, D), F32),
            pltpu.VMEM((LAYERS, PEERS, TOK, D), F32),
            pltpu.SemaphoreType.DMA((LAYERS, 4)),
            pltpu.SemaphoreType.DMA((6,)),
            pltpu.SemaphoreType.DMA((LAYERS, 3)),
            pltpu.SemaphoreType.DMA((LAYERS, 3)),
            pltpu.SemaphoreType.DMA((LAYERS * 10,)),
            pltpu.SemaphoreType.DMA((LAYERS * 10,)),
        ],
        compiler_params=pltpu.CompilerParams(collective_id=0, has_side_effects=True,
                                             vmem_limit_bytes=44 * 1024 * 1024),
        cost_estimate=pl.CostEstimate(flops=400000000, bytes_accessed=32 << 20, transcendentals=0),
    )(*args)


def solution(mesh):
    batch_axes = ('dp', 'col', 'row')

    def local_step(h_first, h_second, start_pos, enc_lens, dec_bias, norm_self, norm_cross, norm_mlp,
                   w_query, w_key, w_value, w_out, w_cquery, w_cout, w_gate, w_up, w_down,
                   self_k, self_v, cross_k, cross_v):
        def flat(cache):
            l, b, t, h, d = cache.shape
            return cache.transpose(0, 1, 3, 4, 2).reshape(l, b, h * d, t)

        def unflat(cache):
            l, b, _, t = cache.shape
            return cache.reshape(l, b, HEADS, 64, t).transpose(0, 1, 4, 2, 3)

        keys, vals = flat(self_k), flat(self_v)
        hidden, new = decode(
            h_first, h_second, start_pos, enc_lens, dec_bias.T, norm_self, norm_cross, norm_mlp,
            w_query, w_key, w_value, w_out, w_cquery, w_cout,
            w_gate.transpose(0, 2, 1), w_up.transpose(0, 2, 1), w_down,
            keys, vals, flat(cross_k), flat(cross_v))
        keys, vals = write_caches(start_pos, new, keys, vals)
        return hidden, unflat(keys), unflat(vals)

    row_spec = P(batch_axes, None)
    seq_spec = P(batch_axes)
    weight_spec = P(None, 'row', 'col')
    cache_spec = P(None, batch_axes)
    in_specs = (row_spec, row_spec, seq_spec, seq_spec, P(), P(), P(), P()) + (weight_spec,) * 9 + (cache_spec,) * 4
    out_specs = (P(None, batch_axes), cache_spec, cache_spec)
    return jax.shard_map(local_step, mesh=mesh, in_specs=in_specs, out_specs=out_specs, check_vma=False)
```

time: 160 us -> 144 us (0.900)
  other arithmetic: 15 us -> 0 us
    select_n x1 -> x0, other arithmetic: 12 us -> none  [write(): return jnp.where(first, rows[:, 0], jnp.where(second, rows[:, 1], cache))]
    pallas_call x1, Pallas kernels: 143 us -> 134 us  [decode(): pl.pallas_call(body, out_shape=(jax.ShapeDtypeStruct((2, SEQS, D), BF16),...]
    pallas_call x0 -> x1, Pallas kernels: none -> 8.4 us  [write_caches(): pl.pallas_call(write_body, grid=(LAYERS * SEQS, 2), out_shape=(jax.ShapeD...]
where the time goes in v2:
time: 144 us
  Pallas kernels  143 us (99%)
    pallas_call x1, Pallas kernels, decode(): pl.pallas_call(body, out_shape=(jax.ShapeDtypeStruct((2, SEQS, D), BF16),...  134 us
    pallas_call x1, Pallas kernels, write_caches(): pl.pallas_call(write_body, grid=(LAYERS * SEQS, 2), out_shape=(jax.ShapeD...  8.4 us

profile of v2, /device:TPU:0, one launch (start us, length us, event | category | flops | bytes accessed | tf_op | source)
XLA Modules:
  0.0 143.9 jit_solution(13194523090223182531)
XLA Ops:
  0.6 0.0 copy-start
  0.6 0.0 copy-start.1
  0.7 0.0 copy-start.2
  0.7 134.2 %shard_map.220 = (bf16[2,2,1024]{2,1,0:T(2,128)(2,1)S(1)}, f32[16,1024]{1,0:T(8,128)S(1)}) custom-call(bf16[2,1024]{1,0:T(2,128)(2,1)} %h0_ref.1, bf16[2,1024]{1,0:T(2,128)(2,1)} %h1_ref.1, s32[2]{0:T(128)} %pos_ref.3, s32[2]{0:T(128)} %len_ref.1, f32[16,32]{1,0:T(8,128)} %bitcast.29, bf16[2,1024]{1,0:T(2,128)(2,1)} %gs_ref.1, bf16[2,1024]{1,0:T(2,128)(2,1)} %gc_ref.1, ...), custom_call_target="tpu_custom_call" | custom-call | flops 400000000 | bytes 33554432 | tf_op jit(solution)/shard_map/pallas_call | solution.py:337
  134.9 0.0 copy-done
  134.9 0.0 copy-done.1
  134.9 0.0 copy-done.2
  134.9 8.4 %shard_map.221 = (bf16[2,2,1024,1024]{3,2,1,0:T(8,128)(2,1)}, bf16[2,2,1024,1024]{3,2,1,0:T(8,128)(2,1)}) custom-call(s32[2]{0:T(128)S(1)} %copy-done.2, f32[16,1024]{1,0:T(8,128)S(1)} %get-tuple-element.8.new_ref, bf16[2,2,1024,1024]{3,2,1,0:T(8,128)(2,1)S(1)} %bitcast.22, bf16[2,2,1024,1024]{3,2,1,0:T(8,128)(2,1)S(1)} %bitcast.24), custom_call_target="tpu_custom_call" | custom-call | flops 1000000 | bytes 33554432 | tf_op jit(solution)/shard_map/pallas_call | solution.py:320
  143.3 0.6 copy.25
Async XLA Ops:
  0.6 134.3 %copy-start = (bf16[2,2,1024,16,64]{2,4,3,1,0:T(8,128)(2,1)S(1)}, bf16[2,2,1024,16,64]{2,4,3,1,0:T(8,128)(2,1)}, u32[]{:S(2)}) copy-start(bf16[2,2,1024,16,64]{2,4,3,1,0:T(8,128)(2,1)} %param.38) | copy-start | bytes 25165828
  0.6 134.3 %copy-start.1 = (bf16[2,2,1024,16,64]{2,4,3,1,0:T(8,128)(2,1)S(1)}, bf16[2,2,1024,16,64]{2,4,3,1,0:T(8,128)(2,1)}, u32[]{:S(2)}) copy-start(bf16[2,2,1024,16,64]{2,4,3,1,0:T(8,128)(2,1)} %param.39) | copy-start | bytes 25165828
  0.7 134.3 %copy-start.2 = (s32[2]{0:T(128)S(1)}, s32[2]{0:T(128)}, u32[]{:S(2)}) copy-start(s32[2]{0:T(128)} %pos_ref.3) | copy-start | bytes 28

commit v3 on v2

--- a/solution.py
+++ b/solution.py
@@ -24,7 +24,24 @@
 E = 512
 FB = 704
 FS = 176
+REPS = 3
 NEG = float("-inf")
+
+SCHEDULE = {
+    0: (('a', 0),),
+    1: (('in', 0, 0, (0, 2)),),
+    2: (('b', 0), ('in', 0, 0, (1, 3))),
+    3: (('c', 0), ('in', 0, 1, (0, 2))),
+    4: (('d', 0), ('a', 1)),
+    5: (('in', 0, 1, (1, 3)), ('e', 0), ('b', 1)),
+    6: (('c', 1),),
+    7: (('d', 1), ('a', 2)),
+    8: (('e', 1), ('b', 2)),
+    9: (('c', 2), ('in', 1, 0, (0, 2))),
+    10: (('d', 2), ('in', 1, 0, (1, 3))),
+    20: (('e', 2), ('in', 1, 1, (0, 2))),
+    21: (('in', 1, 1, (1, 3)),),
+}
 
 
 def nt_dot(a, b):
@@ -41,11 +58,12 @@
          hid_ref, new_ref,
          sk, sv, ck, cv, self_bias, proj_w, gate_w, up_w, down_w,
          a_send, a_recv, p3_send, p3_recv, p1_send, p1_recv,
-         n_send, n_recv, d_send, d_recv,
-         cache_sem, weight_sem, mlp_send_sem, mlp_recv_sem, send_sem, recv_sem):
+         n_send, n_recv, u_send, u_recv,
+         rep, rep_send, rep_recv, cache_sem, weight_sem, mlp_send_sem, mlp_recv_sem, u_send_sem, u_recv_sem, send_sem, recv_sem):
     col = lax.axis_index('col')
     row = lax.axis_index('row')
     me = col * ROWS + row
+    dp = lax.axis_index('dp')
 
     def peer_of(k):
         other = lax.rem(me + k, PEERS)
@@ -56,6 +74,9 @@
         cp = pltpu.make_async_copy(src, proj_w.at[i], weight_sem.at[i])
         cp.start()
         weight_copies.append(cp)
+    cp = pltpu.make_async_copy(wd_hbm, down_w, weight_sem.at[6])
+    cp.start()
+    weight_copies.append(cp)
     cache_copies = []
     for l in range(LAYERS):
         for i, (src, dst) in enumerate(((sk_hbm, sk), (sv_hbm, sv), (ck_hbm, ck), (cv_hbm, cv))):
@@ -67,7 +88,8 @@
     for k in range(1, PEERS):
         _, c, r = peer_of(k)
         pl.semaphore_signal(barrier, inc=1, device_id={'col': c, 'row': r}, device_id_type=pl.DeviceIdType.MESH)
-    pl.semaphore_wait(barrier, PEERS - 1)
+    pl.semaphore_signal(barrier, inc=1, device_id={'dp': 1 - dp}, device_id_type=pl.DeviceIdType.MESH)
+    pl.semaphore_wait(barrier, PEERS)
 
     def exchange(send, recv, idx, by_row):
         def pick(r, other):
@@ -144,35 +166,38 @@
     def project(vec, which, l, e, slot):
         put_act(vec, l, e)
         exchange(a_send.at[l, e], a_recv.at[l, e], l * 10 + slot, True)
+        fill(l * 20 + slot)
         arrive(a_recv.at[l, e], l * 10 + slot)
         prod = nn_dot(gather_act(a_recv.at[l, e]), proj_w[which, l])
         for s in range(PEERS):
             p1_send[l, e - 1, s] = prod[s * TOK:(s + 1) * TOK, :]
         exchange(p1_send.at[l, e - 1], p1_recv.at[l, e - 1], l * 10 + slot + 1, False)
+        fill(l * 20 + slot + 1)
         arrive(p1_recv.at[l, e - 1], l * 10 + slot + 1)
         sums = row_sum(lambda s: p1_recv[l, e - 1, s])
         return round_bf16(jnp.concatenate(sums, axis=1))
 
-    def mlp_copies(l):
-        for i, (src, dst) in enumerate(((wg_hbm, gate_w), (wu_hbm, up_w))):
-            for k in range(ROWS):
-                r = lax.rem(row + k, ROWS)
-                part = src.at[l, pl.ds(pl.multiple_of(r * FS, 16), FS), :]
-                if k == 0:
-                    pltpu.make_async_copy(part, dst.at[l, row], mlp_recv_sem.at[l, i]).start()
-                else:
-                    pltpu.make_async_remote_copy(
-                        src_ref=part, dst_ref=dst.at[l, row], send_sem=mlp_send_sem.at[l, i],
-                        recv_sem=mlp_recv_sem.at[l, i], device_id={'col': col, 'row': r},
-                        device_id_type=pl.DeviceIdType.MESH).start()
-        for k in range(ROWS):
+    def mlp_in(l, i, steps):
+        src, dst = ((wg_hbm, gate_w), (wu_hbm, up_w))[i]
+        for k in steps:
             r = lax.rem(row + k, ROWS)
-            part = wd_hbm.at[l, pl.ds(pl.multiple_of(r * FS, 16), FS), :]
+            part = src.at[l, pl.ds(pl.multiple_of(r * FS, 16), FS), :]
+            if k == 0:
+                pltpu.make_async_copy(part, dst.at[l, row], mlp_recv_sem.at[l, i]).start()
+            else:
+                pltpu.make_async_remote_copy(
+                    src_ref=part, dst_ref=dst.at[l, row], send_sem=mlp_send_sem.at[l, i],
+                    recv_sem=mlp_recv_sem.at[l, i], device_id={'col': col, 'row': r},
+                    device_id_type=pl.DeviceIdType.MESH).start()
+
+    def send_u(l):
+        for k in range(COLS):
+            c = lax.rem(col + k, COLS)
 
             def away():
                 pltpu.make_async_remote_copy(
-                    src_ref=part, dst_ref=down_w.at[l, col], send_sem=mlp_send_sem.at[l, 2],
-                    recv_sem=mlp_recv_sem.at[l, 2], device_id={'col': row, 'row': r},
+                    src_ref=u_send.at[l], dst_ref=u_recv.at[l, row], send_sem=u_send_sem.at[l],
+                    recv_sem=u_recv_sem.at[l], device_id={'col': c, 'row': col},
                     device_id_type=pl.DeviceIdType.MESH).start()
 
             if k == 0:
@@ -180,23 +205,108 @@
 
                 @pl.when(col == row)
                 def _():
-                    pltpu.make_async_copy(part, down_w.at[l, col], mlp_recv_sem.at[l, 2]).start()
+                    pltpu.make_async_copy(u_send.at[l], u_recv.at[l, row], u_recv_sem.at[l]).start()
             else:
                 away()
 
+    own = (wo_hbm, wcq_hbm, wco_hbm)
+    flip = lax.rem(row + 2, ROWS)
+    twin = row + 1 - 2 * lax.rem(row, 2)
+    up_col, down_col = lax.rem(col + 1, COLS), lax.rem(col + COLS - 1, COLS)
+
+    def block_id(dz, other_y):
+        return lax.rem(col + dz, COLS) * ROWS + (flip if other_y else row)
+
+    def pass_on(m, step, src, j, device):
+        pltpu.make_async_remote_copy(
+            src_ref=src, dst_ref=rep.at[m, j], send_sem=rep_send.at[m], recv_sem=rep_recv.at[m, step],
+            device_id=device, device_id_type=pl.DeviceIdType.MESH).start()
+
+    def took(m, step, blocks):
+        part = rep.at[m, pl.ds(0, blocks)]
+        pltpu.make_async_copy(part, part, rep_recv.at[m, step]).wait()
+
+    def rep_a(m):
+        src = own[m].at[1]
+        pltpu.make_async_copy(src, rep.at[m, me], rep_recv.at[m, 0]).start()
+        for device in ({'row': flip}, {'col': up_col}, {'col': down_col}):
+            pass_on(m, 0, src, me, device)
+
+    def rep_b(m):
+        took(m, 0, 4)
+        ahead = block_id(1, False)
+        beside = block_id(0, True)
+        pass_on(m, 1, rep.at[m, beside], beside, {'col': up_col})
+        pass_on(m, 1, rep.at[m, ahead], ahead, {'col': down_col})
+
+        @pl.when(dp == 0)
+        def _():
+            pass_on(m, 1, rep.at[m, ahead], ahead, {'row': flip})
+
+    def rep_c(m):
+        @pl.when(dp == 0)
+        def _():
+            took(m, 1, 3)
+            j = block_id(1, True)
+            pass_on(m, 3, rep.at[m, j], j, {'dp': 1 - dp})
+
+        @pl.when(dp == 1)
+        def _():
+            took(m, 1, 2)
+            j = block_id(2, False)
+            pass_on(m, 2, rep.at[m, j], j, {'row': flip})
+
+    def rep_d(m):
+        @pl.when(dp == 1)
+        def _():
+            took(m, 2, 1)
+            j = block_id(2, True)
+            pass_on(m, 3, rep.at[m, j], j, {'dp': 1 - dp})
+
+    def rep_e(m):
+        took(m, 3, 1)
+        for dz in range(COLS):
+            for other_y in (False, True):
+                j = block_id(dz, other_y)
+                pass_on(m, 4, rep.at[m, j], j, {'row': twin})
+
+    def rep_left(m):
+        part = rep.at[m, pl.ds(0, 15)]
+        pltpu.make_async_copy(part, part, rep_send.at[m]).wait()
+
+    def local_project(vec, m):
+        took(m, 4, 8)
+        sums = []
+        for c in range(COLS):
+            acc = nn_dot(vec[:, 0:256], rep[m, c * ROWS])
+            for r in range(1, ROWS):
+                acc = acc + nn_dot(vec[:, r * 256:(r + 1) * 256], rep[m, c * ROWS + r])
+            sums.append(acc)
+        return round_bf16(jnp.concatenate(sums, axis=1))
+
+    work = SCHEDULE
+
+    def fill(slot):
+        for name, *what in work.get(slot, ()):
+            {'in': mlp_in, 'a': rep_a, 'b': rep_b, 'c': rep_c, 'd': rep_d, 'e': rep_e}[name](*what)
+
     def mlp_arrive(l):
-        for i, dst in enumerate((gate_w, up_w, down_w)):
+        for i, dst in enumerate((gate_w, up_w)):
             pltpu.make_async_copy(dst.at[l], dst.at[l], mlp_recv_sem.at[l, i]).wait()
 
     def mlp_left(l):
-        for i, dst in enumerate((gate_w, up_w, down_w)):
+        for i, dst in enumerate((gate_w, up_w)):
             part = dst.at[l, pl.ds(0, ROWS - 1)]
             pltpu.make_async_copy(part, part, mlp_send_sem.at[l, i]).wait()
+        part = u_recv.at[l, pl.ds(0, COLS - 1)]
+        pltpu.make_async_copy(part, part, u_send_sem.at[l]).wait()
 
         @pl.when(col != row)
         def _():
-            part = down_w.at[l, 0]
-            pltpu.make_async_copy(part, part, mlp_send_sem.at[l, 2]).wait()
+            pltpu.make_async_copy(u_recv.at[l, 0], u_recv.at[l, 0], u_send_sem.at[l]).wait()
+
+    def apply(vec, which, l, e, slot):
+        return project(vec, which, l, e, slot) if l == 0 else local_project(vec, which - 3)
 
     x = jnp.concatenate([h0_ref[...].astype(F32), h1_ref[...].astype(F32)], axis=0)
     for l in range(LAYERS):
@@ -204,6 +314,7 @@
         n = rms(x, gs_ref[l:l + 1, :]).astype(BF16)
         put_act(n, l, 0)
         exchange(a_send.at[l, 0], a_recv.at[l, 0], base, True)
+        fill(l * 20)
         if l == 0:
             build_bias()
             for cp in weight_copies:
@@ -215,7 +326,7 @@
             for s in range(PEERS):
                 p3_send[l, s, :, i * 256:(i + 1) * 256] = prod[s * TOK:(s + 1) * TOK, :]
         exchange(p3_send.at[l], p3_recv.at[l], base + 1, False)
-        mlp_copies(l)
+        fill(l * 20 + 1)
         arrive(p3_recv.at[l], base + 1)
         sums = row_sum(lambda s: p3_recv[l, s])
         q4, k4, v4 = (round_bf16(jnp.concatenate([sm[:, i * 256:(i + 1) * 256] for sm in sums], axis=1))
@@ -238,10 +349,10 @@
             total = jnp.sum(e_old, axis=1, keepdims=True) + jnp.sum(e_new, axis=1, keepdims=True)
             mixed = nt_dot((e_old / total).astype(BF16), sv[l, b]) + nn_dot((e_new / total).astype(BF16), vn)
             pieces.append(fold_heads(mixed))
-        x = x + project(join_tokens(pieces).astype(BF16), 3, l, 1, 2)
+        x = x + apply(join_tokens(pieces).astype(BF16), 3, l, 1, 2)
 
         n = rms(x, gc_ref[l:l + 1, :]).astype(BF16)
-        q4 = project(n, 4, l, 2, 4)
+        q4 = apply(n, 4, l, 2, 4)
         cache_copies[l * 4 + 2].wait()
         cache_copies[l * 4 + 3].wait()
         pieces = []
@@ -251,10 +362,11 @@
             ex = jnp.exp(sc - jnp.max(sc, axis=1, keepdims=True))
             probs = (ex / jnp.sum(ex, axis=1, keepdims=True)).astype(BF16)
             pieces.append(fold_heads(nt_dot(probs, cv[l, b])))
-        x = x + project(join_tokens(pieces).astype(BF16), 5, l, 3, 6)
+        x = x + apply(join_tokens(pieces).astype(BF16), 5, l, 3, 6)
 
         n_send[l, 0] = rms(x, gm_ref[l:l + 1, :]).astype(BF16)
         exchange(n_send.at[l], n_recv.at[l], base + 8, None)
+        fill(l * 20 + 8)
         mlp_arrive(l)
         arrive(n_recv.at[l], base + 8)
         act = gather_act(n_recv.at[l])
@@ -263,17 +375,20 @@
         for r in range(1, ROWS):
             gate = gate + nt_dot(act[:, r * 256:(r + 1) * 256], gate_w[l, r])
             up = up + nt_dot(act[:, r * 256:(r + 1) * 256], up_w[l, r])
-        u = (jax.nn.silu(round_bf16(gate)) * round_bf16(up)).astype(BF16)
-        for c in range(COLS):
-            prod = nn_dot(u, down_w[l, c])
-            for s in range(PEERS):
-                d_send[l, s, :, c * 256:(c + 1) * 256] = prod[s * TOK:(s + 1) * TOK, :]
-        exchange(d_send.at[l], d_recv.at[l], base + 9, False)
-        arrive(d_recv.at[l], base + 9)
-        terms = [d_recv[l, s] for s in range(PEERS)]
-        while len(terms) > 1:
-            terms = [terms[i] + terms[i + 1] for i in range(0, len(terms), 2)]
-        x = x + round_bf16(terms[0])
+        u_send[l] = (jax.nn.silu(round_bf16(gate)) * round_bf16(up)).astype(BF16)
+        send_u(l)
+        fill(l * 20 + 9)
+        pltpu.make_async_copy(u_recv.at[l], u_recv.at[l], u_recv_sem.at[l]).wait()
+        prod = nn_dot(u_recv[l, 0], down_w[l, 0:FS])
+        for r in range(1, ROWS):
+            prod = prod + nn_dot(u_recv[l, r], down_w[l, r * FS:(r + 1) * FS])
+        for s in range(PEERS):
+            p1_send[l, 3, s] = prod[s * TOK:(s + 1) * TOK, :]
+        exchange(p1_send.at[l, 3], p1_recv.at[l, 3], l * 10 + 9, False)
+        fill(l * 20 + 10)
+        arrive(p1_recv.at[l, 3], l * 10 + 9)
+        sums = row_sum(lambda s: p1_recv[l, 3, s])
+        x = x + round_bf16(jnp.concatenate(sums, axis=1))
 
     hid_ref[0] = x[0:2].astype(BF16)
     hid_ref[1] = x[2:4].astype(BF16)
@@ -281,12 +396,14 @@
         base = l * 10
         left(a_recv.at[l, 0], base)
         left(p3_recv.at[l], base + 1)
-        for e in (1, 2, 3):
+        for e in (1, 2, 3) if l == 0 else ():
             left(a_recv.at[l, e], base + 2 * e)
             left(p1_recv.at[l, e - 1], base + 2 * e + 1)
         left(n_recv.at[l], base + 8)
-        left(d_recv.at[l], base + 9)
+        left(p1_recv.at[l, 3], base + 9)
         mlp_left(l)
+    for m in range(REPS):
+        rep_left(m)
 
 
 def write_body(pos_ref, new_ref, k_ref, v_ref, ko_ref, vo_ref, cols):
@@ -349,21 +466,26 @@
             pltpu.VMEM((6, LAYERS, 256, 256), BF16),
             pltpu.VMEM((LAYERS, ROWS, FS, 256), BF16),
             pltpu.VMEM((LAYERS, ROWS, FS, 256), BF16),
-            pltpu.VMEM((LAYERS, COLS, FS, 256), BF16),
+            pltpu.VMEM((LAYERS, FB, 256), BF16),
             pltpu.VMEM((LAYERS, 4, ROWS, TOK, 256), BF16),
             pltpu.VMEM((LAYERS, 4, PEERS, TOK, 256), BF16),
             pltpu.VMEM((LAYERS, PEERS, TOK, 768), F32),
             pltpu.VMEM((LAYERS, PEERS, TOK, 768), F32),
-            pltpu.VMEM((LAYERS, 3, PEERS, TOK, 256), F32),
-            pltpu.VMEM((LAYERS, 3, PEERS, TOK, 256), F32),
+            pltpu.VMEM((LAYERS, 4, PEERS, TOK, 256), F32),
+            pltpu.VMEM((LAYERS, 4, PEERS, TOK, 256), F32),
             pltpu.VMEM((LAYERS, 1, TOK, D), BF16),
             pltpu.VMEM((LAYERS, PEERS, TOK, D), BF16),
-            pltpu.VMEM((LAYERS, PEERS, TOK, D), F32),
-            pltpu.VMEM((LAYERS, PEERS, TOK, D), F32),
+            pltpu.VMEM((LAYERS, PEERS * TOK, FS), BF16),
+            pltpu.VMEM((LAYERS, ROWS, PEERS * TOK, FS), BF16),
+            pltpu.VMEM((REPS, PEERS, 256, 256), BF16),
+            pltpu.SemaphoreType.DMA((REPS,)),
+            pltpu.SemaphoreType.DMA((REPS, 5)),
             pltpu.SemaphoreType.DMA((LAYERS, 4)),
-            pltpu.SemaphoreType.DMA((6,)),
-            pltpu.SemaphoreType.DMA((LAYERS, 3)),
-            pltpu.SemaphoreType.DMA((LAYERS, 3)),
+            pltpu.SemaphoreType.DMA((7,)),
+            pltpu.SemaphoreType.DMA((LAYERS, 2)),
+            pltpu.SemaphoreType.DMA((LAYERS, 2)),
+            pltpu.SemaphoreType.DMA((LAYERS,)),
+            pltpu.SemaphoreType.DMA((LAYERS,)),
             pltpu.SemaphoreType.DMA((LAYERS * 10,)),
             pltpu.SemaphoreType.DMA((LAYERS * 10,)),
         ],

time: 144 us -> 120 us (0.83)
  Pallas kernels: 143 us -> 118 us
    pallas_call x1, Pallas kernels: 134 us -> 110 us  [decode(): pl.pallas_call(body, out_shape=(jax.ShapeDtypeStruct((2, SEQS, D), BF16),...]
where the time goes in v3:
time: 120 us; the launch traced here: 119 us
  Pallas kernels  118 us (98%)
    pallas_call x1, Pallas kernels, decode(): pl.pallas_call(body, out_shape=(jax.ShapeDtypeStruct((2, SEQS, D), BF16),...  110 us
    pallas_call x1, Pallas kernels, write_caches(): pl.pallas_call(write_body, grid=(LAYERS * SEQS, 2), out_shape=(jax.ShapeD...  8.4 us

profile of v3, /device:TPU:0, one launch (start us, length us, event | category | flops | bytes accessed | tf_op | source)
XLA Modules:
  0.0 119.5 jit_solution(15482324284798960824)
XLA Ops:
  0.6 0.0 copy-start
  0.6 0.0 copy-start.1
  0.7 0.0 copy-start.2
  0.7 109.7 %shard_map.220 = (bf16[2,2,1024]{2,1,0:T(2,128)(2,1)S(1)}, f32[16,1024]{1,0:T(8,128)S(1)}) custom-call(bf16[2,1024]{1,0:T(2,128)(2,1)} %h0_ref.1, bf16[2,1024]{1,0:T(2,128)(2,1)} %h1_ref.1, s32[2]{0:T(128)} %pos_ref.3, s32[2]{0:T(128)} %len_ref.1, f32[16,32]{1,0:T(8,128)} %bitcast.29, bf16[2,1024]{1,0:T(2,128)(2,1)} %gs_ref.1, bf16[2,1024]{1,0:T(2,128)(2,1)} %gc_ref.1, ...), custom_call_target="tpu_custom_call" | custom-call | flops 400000000 | bytes 33554432 | tf_op jit(solution)/shard_map/pallas_call | solution.py:454
  110.4 0.0 copy-done
  110.4 0.0 copy-done.1
  110.4 0.0 copy-done.2
  110.5 8.4 %shard_map.221 = (bf16[2,2,1024,1024]{3,2,1,0:T(8,128)(2,1)}, bf16[2,2,1024,1024]{3,2,1,0:T(8,128)(2,1)}) custom-call(s32[2]{0:T(128)S(1)} %copy-done.2, f32[16,1024]{1,0:T(8,128)S(1)} %get-tuple-element.8.new_ref, bf16[2,2,1024,1024]{3,2,1,0:T(8,128)(2,1)S(1)} %bitcast.22, bf16[2,2,1024,1024]{3,2,1,0:T(8,128)(2,1)S(1)} %bitcast.24), custom_call_target="tpu_custom_call" | custom-call | flops 1000000 | bytes 33554432 | tf_op jit(solution)/shard_map/pallas_call | solution.py:437
  118.9 0.6 copy.25
Async XLA Ops:
  0.6 109.8 %copy-start = (bf16[2,2,1024,16,64]{2,4,3,1,0:T(8,128)(2,1)S(1)}, bf16[2,2,1024,16,64]{2,4,3,1,0:T(8,128)(2,1)}, u32[]{:S(2)}) copy-start(bf16[2,2,1024,16,64]{2,4,3,1,0:T(8,128)(2,1)} %param.38) | copy-start | bytes 25165828
  0.6 109.8 %copy-start.1 = (bf16[2,2,1024,16,64]{2,4,3,1,0:T(8,128)(2,1)S(1)}, bf16[2,2,1024,16,64]{2,4,3,1,0:T(8,128)(2,1)}, u32[]{:S(2)}) copy-start(bf16[2,2,1024,16,64]{2,4,3,1,0:T(8,128)(2,1)} %param.39) | copy-start | bytes 25165828
  0.7 109.8 %copy-start.2 = (s32[2]{0:T(128)S(1)}, s32[2]{0:T(128)}, u32[]{:S(2)}) copy-start(s32[2]{0:T(128)} %pos_ref.3) | copy-start | bytes 28

commit v4 on v3

--- a/solution.py
+++ b/solution.py
@@ -28,19 +28,20 @@
 NEG = float("-inf")
 
 SCHEDULE = {
-    0: (('a', 0),),
+    0: (('z', 0, 1), ('y', 0, 0)),
     1: (('in', 0, 0, (0, 2)),),
-    2: (('b', 0), ('in', 0, 0, (1, 3))),
-    3: (('c', 0), ('in', 0, 1, (0, 2))),
-    4: (('d', 0), ('a', 1)),
-    5: (('in', 0, 1, (1, 3)), ('e', 0), ('b', 1)),
-    6: (('c', 1),),
-    7: (('d', 1), ('a', 2)),
-    8: (('e', 1), ('b', 2)),
-    9: (('c', 2), ('in', 1, 0, (0, 2))),
-    10: (('d', 2), ('in', 1, 0, (1, 3))),
-    20: (('e', 2), ('in', 1, 1, (0, 2))),
-    21: (('in', 1, 1, (1, 3)),),
+    2: (('z', 0, 2), ('y', 0, 1), ('in', 0, 0, (1, 3))),
+    3: (('z', 0, 3), ('in', 0, 1, (0, 2))),
+    4: (('y', 0, 2), ('z', 1, 1), ('y', 1, 0)),
+    5: (('y', 0, 3), ('z', 1, 2), ('in', 0, 1, (1, 3))),
+    6: (('z', 1, 3), ('y', 1, 1), ('x', 0)),
+    7: (('y', 1, 2), ('z', 2, 1), ('y', 2, 0)),
+    8: (('e', 0), ('y', 1, 3), ('z', 2, 3)),
+    9: (('y', 2, 1), ('x', 1), ('in', 1, 0, (0, 2))),
+    10: (('z', 2, 2), ('y', 2, 3), ('in', 1, 0, (1, 3))),
+    20: (('e', 1), ('y', 2, 2), ('in', 1, 1, (0, 2))),
+    21: (('x', 2), ('in', 1, 1, (1, 3))),
+    50: (('e', 2),),
 }
 
 
@@ -212,70 +213,58 @@
     own = (wo_hbm, wcq_hbm, wco_hbm)
     flip = lax.rem(row + 2, ROWS)
     twin = row + 1 - 2 * lax.rem(row, 2)
-    up_col, down_col = lax.rem(col + 1, COLS), lax.rem(col + COLS - 1, COLS)
-
-    def block_id(dz, other_y):
-        return lax.rem(col + dz, COLS) * ROWS + (flip if other_y else row)
-
-    def pass_on(m, step, src, j, device):
+    first_row = pl.multiple_of(dp * 128, 128)
+
+    def half(m, j):
+        return rep.at[m, j, pl.ds(first_row, 128), :]
+
+    def pass_on(m, step, src, dst, device):
         pltpu.make_async_remote_copy(
-            src_ref=src, dst_ref=rep.at[m, j], send_sem=rep_send.at[m], recv_sem=rep_recv.at[m, step],
+            src_ref=src, dst_ref=dst, send_sem=rep_send.at[m], recv_sem=rep_recv.at[m, step],
             device_id=device, device_id_type=pl.DeviceIdType.MESH).start()
 
     def took(m, step, blocks):
         part = rep.at[m, pl.ds(0, blocks)]
         pltpu.make_async_copy(part, part, rep_recv.at[m, step]).wait()
 
-    def rep_a(m):
-        src = own[m].at[1]
-        pltpu.make_async_copy(src, rep.at[m, me], rep_recv.at[m, 0]).start()
-        for device in ({'row': flip}, {'col': up_col}, {'col': down_col}):
-            pass_on(m, 0, src, me, device)
-
-    def rep_b(m):
-        took(m, 0, 4)
-        ahead = block_id(1, False)
-        beside = block_id(0, True)
-        pass_on(m, 1, rep.at[m, beside], beside, {'col': up_col})
-        pass_on(m, 1, rep.at[m, ahead], ahead, {'col': down_col})
-
-        @pl.when(dp == 0)
-        def _():
-            pass_on(m, 1, rep.at[m, ahead], ahead, {'row': flip})
-
-    def rep_c(m):
-        @pl.when(dp == 0)
-        def _():
-            took(m, 1, 3)
-            j = block_id(1, True)
-            pass_on(m, 3, rep.at[m, j], j, {'dp': 1 - dp})
-
-        @pl.when(dp == 1)
-        def _():
-            took(m, 1, 2)
-            j = block_id(2, False)
-            pass_on(m, 2, rep.at[m, j], j, {'row': flip})
-
-    def rep_d(m):
-        @pl.when(dp == 1)
-        def _():
-            took(m, 2, 1)
-            j = block_id(2, True)
-            pass_on(m, 3, rep.at[m, j], j, {'dp': 1 - dp})
+    def took_halves(m, step, halves):
+        part = rep.at[m, pl.ds(0, halves), pl.ds(0, 128), :]
+        pltpu.make_async_copy(part, part, rep_recv.at[m, step]).wait()
+
+    def rep_z(m, k):
+        if k == 1:
+            pltpu.make_async_copy(own[m].at[1], rep.at[m, me], rep_recv.at[m, 6]).start()
+        pass_on(m, k - 1, own[m].at[1, pl.ds(first_row, 128), :], half(m, me), {'col': lax.rem(col + k, COLS)})
+
+    def rep_y(m, k):
+        j = lax.rem(col + COLS - k, COLS) * ROWS + row
+        if k == 0:
+            pass_on(m, 3, own[m].at[1, pl.ds(first_row, 128), :], half(m, j), {'row': flip})
+        else:
+            took_halves(m, k - 1, 1)
+            pass_on(m, 3, half(m, j), half(m, j), {'row': flip})
+            pass_on(m, 4, half(m, j), half(m, j), {'dp': 1 - dp})
+
+    def rep_x(m):
+        took_halves(m, 3, 4)
+        for c in range(COLS):
+            j = c * ROWS + flip
+            pass_on(m, 4, half(m, j), half(m, j), {'dp': 1 - dp})
 
     def rep_e(m):
-        took(m, 3, 1)
-        for dz in range(COLS):
-            for other_y in (False, True):
-                j = block_id(dz, other_y)
-                pass_on(m, 4, rep.at[m, j], j, {'row': twin})
+        took_halves(m, 4, 7)
+        took(m, 6, 1)
+        for c in range(COLS):
+            for r in (row, flip):
+                j = c * ROWS + r
+                pass_on(m, 5, rep.at[m, j], rep.at[m, j], {'row': twin})
 
     def rep_left(m):
         part = rep.at[m, pl.ds(0, 15)]
         pltpu.make_async_copy(part, part, rep_send.at[m]).wait()
 
     def local_project(vec, m):
-        took(m, 4, 8)
+        took(m, 5, 8)
         sums = []
         for c in range(COLS):
             acc = nn_dot(vec[:, 0:256], rep[m, c * ROWS])
@@ -288,7 +277,7 @@
 
     def fill(slot):
         for name, *what in work.get(slot, ()):
-            {'in': mlp_in, 'a': rep_a, 'b': rep_b, 'c': rep_c, 'd': rep_d, 'e': rep_e}[name](*what)
+            {'in': mlp_in, 'z': rep_z, 'y': rep_y, 'x': rep_x, 'e': rep_e}[name](*what)
 
     def mlp_arrive(l):
         for i, dst in enumerate((gate_w, up_w)):
@@ -353,6 +342,7 @@
 
         n = rms(x, gc_ref[l:l + 1, :]).astype(BF16)
         q4 = apply(n, 4, l, 2, 4)
+        fill(l * 20 + 30)
         cache_copies[l * 4 + 2].wait()
         cache_copies[l * 4 + 3].wait()
         pieces = []
@@ -406,42 +396,65 @@
         rep_left(m)
 
 
-def write_body(pos_ref, new_ref, k_ref, v_ref, ko_ref, vo_ref, cols):
-    i = pl.program_id(0)
-    half = pl.program_id(1)
-
-    @pl.when((i == 0) & (half == 0))
-    def _():
-        cols[...] = jnp.transpose(new_ref[...])
-
-    b = lax.rem(i, SEQS)
-    l = i // SEQS
-    p = pos_ref[b]
-    lanes = lax.broadcasted_iota(jnp.int32, (512, 128), 1)
-    pick = lax.broadcasted_iota(jnp.int32, (512, 16), 1)
-    mine = cols[pl.ds(pl.multiple_of(half * 512, 512), 512), :]
-    for kv, (src, dst) in enumerate(((k_ref, ko_ref), (v_ref, vo_ref))):
-        dst[...] = src[...]
+def write_body(pos_ref, new_ref, k_ref, v_ref, ko_ref, vo_ref, cols, patch, sem):
+    lanes = lax.broadcasted_iota(jnp.int32, (D, 128), 1)
+    blocks = [(l, b, kv) for l in range(LAYERS) for b in range(SEQS) for kv in range(2)]
+
+    def refs(kv):
+        return (k_ref, ko_ref) if kv == 0 else (v_ref, vo_ref)
+
+    def tiles(l, b, kv, put):
+        first, second = pos_ref[b] // 128, (pos_ref[b] + 1) // 128
+        src, dst = refs(kv)
+        for i in range(T // 128):
+            out = dst.at[l, b, :, pl.ds(i * 128, 128)]
+            put(i, first, second, src.at[l, b, :, pl.ds(i * 128, 128)], out)
+
+    for l, b, kv in blocks:
+        def plain(i, first, second, src, out):
+            @pl.when((first != i) & (second != i))
+            def _():
+                pltpu.make_async_copy(src, out, sem.at[l, b, kv]).start()
+
+        tiles(l, b, kv, plain)
+
+    cols[...] = jnp.transpose(new_ref[...])
+    for l, b, kv in blocks:
+        p = pos_ref[b]
         at = l * 8 + kv * TOK + b
-        first = jnp.sum(jnp.where(pick == at, mine, 0.0), axis=1, keepdims=True)
-        second = jnp.sum(jnp.where(pick == at + 2, mine, 0.0), axis=1, keepdims=True)
+        src, _ = refs(kv)
         for q in range(2):
             start = pl.multiple_of(((p + q) // 128) * 128, 128)
-            old = src[0, 0, :, pl.ds(start, 128)].astype(F32)
-            fresh = jnp.where(lanes + start == p, first, jnp.where(lanes + start == p + 1, second, old))
-            dst[0, 0, :, pl.ds(start, 128)] = fresh.astype(BF16)
+            old = src[l, b, :, pl.ds(start, 128)].astype(F32)
+            fresh = jnp.where(lanes + start == p, cols[:, at:at + 1],
+                              jnp.where(lanes + start == p + 1, cols[:, at + 2:at + 3], old))
+            patch[l, b, kv, q] = fresh.astype(BF16)
+
+        def changed(i, first, second, src, out):
+            @pl.when(first == i)
+            def _():
+                pltpu.make_async_copy(patch.at[l, b, kv, 0], out, sem.at[l, b, kv]).start()
+
+            @pl.when((second == i) & (first != i))
+            def _():
+                pltpu.make_async_copy(patch.at[l, b, kv, 1], out, sem.at[l, b, kv]).start()
+
+        tiles(l, b, kv, changed)
+    for l, b, kv in blocks:
+        src, dst = refs(kv)
+        pltpu.make_async_copy(src.at[l, b], dst.at[l, b], sem.at[l, b, kv]).wait()
 
 
 def write_caches(pos, new, k, v):
-    block = pl.BlockSpec((1, 1, 512, T), lambda i, j: (i // SEQS, i % SEQS, j, 0))
+    vmem = pl.BlockSpec(memory_space=pltpu.VMEM)
     return pl.pallas_call(
         write_body,
-        grid=(LAYERS * SEQS, 2),
         out_shape=(jax.ShapeDtypeStruct(k.shape, BF16),) * 2,
-        in_specs=[pl.BlockSpec(memory_space=pltpu.SMEM), pl.BlockSpec((16, D), lambda i, j: (0, 0)), block, block],
-        out_specs=(block, block),
-        scratch_shapes=[pltpu.VMEM((D, 16), F32)],
-        compiler_params=pltpu.CompilerParams(vmem_limit_bytes=14 * 1024 * 1024),
+        in_specs=[pl.BlockSpec(memory_space=pltpu.SMEM), vmem, vmem, vmem],
+        out_specs=(pl.BlockSpec(memory_space=pltpu.HBM),) * 2,
+        scratch_shapes=[pltpu.VMEM((D, 16), F32), pltpu.VMEM((LAYERS, SEQS, 2, 2, D, 128), BF16),
+                        pltpu.SemaphoreType.DMA((LAYERS, SEQS, 2))],
+        compiler_params=pltpu.CompilerParams(vmem_limit_bytes=28 * 1024 * 1024),
         cost_estimate=pl.CostEstimate(flops=1000000, bytes_accessed=32 << 20, transcendentals=0),
     )(pos, new, k, v)
 
@@ -479,7 +492,7 @@
             pltpu.VMEM((LAYERS, ROWS, PEERS * TOK, FS), BF16),
             pltpu.VMEM((REPS, PEERS, 256, 256), BF16),
             pltpu.SemaphoreType.DMA((REPS,)),
-            pltpu.SemaphoreType.DMA((REPS, 5)),
+            pltpu.SemaphoreType.DMA((REPS, 7)),
             pltpu.SemaphoreType.DMA((LAYERS, 4)),
             pltpu.SemaphoreType.DMA((7,)),
             pltpu.SemaphoreType.DMA((LAYERS, 2)),

time: 120 us -> 109 us (0.908)
  Pallas kernels: 118 us -> 108 us
    pallas_call x1, Pallas kernels: 110 us -> 101 us  [decode(): pl.pallas_call(body, out_shape=(jax.ShapeDtypeStruct((2, SEQS, D), BF16),...]
    pallas_call x1, Pallas kernels: 8.4 us -> 7.01 us  [write_caches(): pl.pallas_call(write_body, out_shape=(jax.ShapeDtypeStruct(k.shape, BF16)...]
where the time goes in v4:
time: 109 us
  Pallas kernels  108 us (99%)
    pallas_call x1, Pallas kernels, decode(): pl.pallas_call(body, out_shape=(jax.ShapeDtypeStruct((2, SEQS, D), BF16),...  101 us
    pallas_call x1, Pallas kernels, write_caches(): pl.pallas_call(write_body, out_shape=(jax.ShapeDtypeStruct(k.shape, BF16)...  7.01 us

profile of v4, /device:TPU:0, one launch (start us, length us, event | category | flops | bytes accessed | tf_op | source)
XLA Modules:
  0.0 109.0 jit_solution(12592812779883924045)
XLA Ops:
  0.6 0.0 copy-start
  0.6 0.0 copy-start.1
  0.7 0.0 copy-start.2
  0.7 100.7 %shard_map.220 = (bf16[2,2,1024]{2,1,0:T(2,128)(2,1)S(1)}, f32[16,1024]{1,0:T(8,128)S(1)}) custom-call(bf16[2,1024]{1,0:T(2,128)(2,1)} %h0_ref.1, bf16[2,1024]{1,0:T(2,128)(2,1)} %h1_ref.1, s32[2]{0:T(128)} %pos_ref.3, s32[2]{0:T(128)} %len_ref.1, f32[16,32]{1,0:T(8,128)} %bitcast.29, bf16[2,1024]{1,0:T(2,128)(2,1)} %gs_ref.1, bf16[2,1024]{1,0:T(2,128)(2,1)} %gc_ref.1, ...), custom_call_target="tpu_custom_call" | custom-call | flops 400000000 | bytes 33554432 | tf_op jit(solution)/shard_map/pallas_call | solution.py:467
  101.4 0.0 copy-done
  101.4 0.0 copy-done.1
  101.4 0.0 copy-done.2
  101.4 7.0 %shard_map.221 = (bf16[2,2,1024,1024]{3,2,1,0:T(8,128)(2,1)}, bf16[2,2,1024,1024]{3,2,1,0:T(8,128)(2,1)}) custom-call(s32[2]{0:T(128)S(1)} %copy-done.2, f32[16,1024]{1,0:T(8,128)S(1)} %get-tuple-element.8.new_ref, bf16[2,2,1024,1024]{3,2,1,0:T(8,128)(2,1)S(1)} %bitcast.22, bf16[2,2,1024,1024]{3,2,1,0:T(8,128)(2,1)S(1)} %bitcast.24), custom_call_target="tpu_custom_call" | custom-call | flops 1000000 | bytes 33554432 | tf_op jit(solution)/shard_map/pallas_call | solution.py:450
  108.4 0.6 copy.25
Async XLA Ops:
  0.6 100.8 %copy-start = (bf16[2,2,1024,16,64]{2,4,3,1,0:T(8,128)(2,1)S(1)}, bf16[2,2,1024,16,64]{2,4,3,1,0:T(8,128)(2,1)}, u32[]{:S(2)}) copy-start(bf16[2,2,1024,16,64]{2,4,3,1,0:T(8,128)(2,1)} %param.38) | copy-start | bytes 25165828
  0.6 100.8 %copy-start.1 = (bf16[2,2,1024,16,64]{2,4,3,1,0:T(8,128)(2,1)S(1)}, bf16[2,2,1024,16,64]{2,4,3,1,0:T(8,128)(2,1)}, u32[]{:S(2)}) copy-start(bf16[2,2,1024,16,64]{2,4,3,1,0:T(8,128)(2,1)} %param.39) | copy-start | bytes 25165828
  0.7 100.8 %copy-start.2 = (s32[2]{0:T(128)S(1)}, s32[2]{0:T(128)}, u32[]{:S(2)}) copy-start(s32[2]{0:T(128)} %pos_ref.3) | copy-start | bytes 28

commit v5 on v4

--- a/solution.py
+++ b/solution.py
@@ -24,24 +24,22 @@
 E = 512
 FB = 704
 FS = 176
-REPS = 3
+REPS = 4
 NEG = float("-inf")
 
 SCHEDULE = {
-    0: (('z', 0, 1), ('y', 0, 0)),
-    1: (('in', 0, 0, (0, 2)),),
-    2: (('z', 0, 2), ('y', 0, 1), ('in', 0, 0, (1, 3))),
-    3: (('z', 0, 3), ('in', 0, 1, (0, 2))),
-    4: (('y', 0, 2), ('z', 1, 1), ('y', 1, 0)),
-    5: (('y', 0, 3), ('z', 1, 2), ('in', 0, 1, (1, 3))),
-    6: (('z', 1, 3), ('y', 1, 1), ('x', 0)),
-    7: (('y', 1, 2), ('z', 2, 1), ('y', 2, 0)),
-    8: (('e', 0), ('y', 1, 3), ('z', 2, 3)),
-    9: (('y', 2, 1), ('x', 1), ('in', 1, 0, (0, 2))),
-    10: (('z', 2, 2), ('y', 2, 3), ('in', 1, 0, (1, 3))),
-    20: (('e', 1), ('y', 2, 2), ('in', 1, 1, (0, 2))),
-    21: (('x', 2), ('in', 1, 1, (1, 3))),
-    50: (('e', 2),),
+    0: (('z', 0, 1), ('z', 0, 3), ('y', 0, 0), ('in', 0, 0, (0, 2))),
+    1: (('y', 0, 1), ('y', 0, 3), ('in', 0, 0, (1, 3))),
+    2: (('z', 0, 2), ('in', 0, 1, (0, 2)), ('y', 1, 0)),
+    3: (('y', 0, 2), ('in', 0, 1, (1, 3)), ('z', 1, 1), ('z', 1, 3)),
+    4: (('x', 0), ('y', 1, 1), ('y', 1, 3), ('z', 1, 2)),
+    5: (('y', 1, 2), ('y', 2, 0), ('z', 2, 1), ('z', 2, 3)),
+    100: (('e', 0), ('y', 2, 1), ('y', 2, 3), ('z', 2, 2), ('x', 1)),
+    8: (('y', 2, 2), ('y', 3, 0), ('z', 3, 1), ('z', 3, 3)),
+    9: (('y', 3, 1), ('y', 3, 3), ('x', 2), ('z', 3, 2)),
+    10: (('y', 3, 2), ('in', 1, 0, (0, 2)), ('e', 1)),
+    20: (('x', 3), ('in', 1, 0, (1, 3)), ('e', 2)),
+    21: (('e', 3), ('in', 1, 1, (0, 2)), ('in', 1, 1, (1, 3))),
 }
 
 
@@ -210,7 +208,7 @@
             else:
                 away()
 
-    own = (wo_hbm, wcq_hbm, wco_hbm)
+    own = (wco_hbm.at[0], wo_hbm.at[1], wcq_hbm.at[1], wco_hbm.at[1])
     flip = lax.rem(row + 2, ROWS)
     twin = row + 1 - 2 * lax.rem(row, 2)
     first_row = pl.multiple_of(dp * 128, 128)
@@ -233,13 +231,13 @@
 
     def rep_z(m, k):
         if k == 1:
-            pltpu.make_async_copy(own[m].at[1], rep.at[m, me], rep_recv.at[m, 6]).start()
-        pass_on(m, k - 1, own[m].at[1, pl.ds(first_row, 128), :], half(m, me), {'col': lax.rem(col + k, COLS)})
+            pltpu.make_async_copy(own[m], rep.at[m, me], rep_recv.at[m, 6]).start()
+        pass_on(m, k - 1, own[m].at[pl.ds(first_row, 128), :], half(m, me), {'col': lax.rem(col + k, COLS)})
 
     def rep_y(m, k):
         j = lax.rem(col + COLS - k, COLS) * ROWS + row
         if k == 0:
-            pass_on(m, 3, own[m].at[1, pl.ds(first_row, 128), :], half(m, j), {'row': flip})
+            pass_on(m, 3, own[m].at[pl.ds(first_row, 128), :], half(m, j), {'row': flip})
         else:
             took_halves(m, k - 1, 1)
             pass_on(m, 3, half(m, j), half(m, j), {'row': flip})
@@ -295,7 +293,8 @@
             pltpu.make_async_copy(u_recv.at[l, 0], u_recv.at[l, 0], u_send_sem.at[l]).wait()
 
     def apply(vec, which, l, e, slot):
-        return project(vec, which, l, e, slot) if l == 0 else local_project(vec, which - 3)
+        m = {(0, 5): 0, (1, 3): 1, (1, 4): 2, (1, 5): 3}.get((l, which))
+        return project(vec, which, l, e, slot) if m is None else local_project(vec, m)
 
     x = jnp.concatenate([h0_ref[...].astype(F32), h1_ref[...].astype(F32)], axis=0)
     for l in range(LAYERS):
@@ -342,7 +341,7 @@
 
         n = rms(x, gc_ref[l:l + 1, :]).astype(BF16)
         q4 = apply(n, 4, l, 2, 4)
-        fill(l * 20 + 30)
+        fill(l * 20 + 100)
         cache_copies[l * 4 + 2].wait()
         cache_copies[l * 4 + 3].wait()
         pieces = []
@@ -386,7 +385,7 @@
         base = l * 10
         left(a_recv.at[l, 0], base)
         left(p3_recv.at[l], base + 1)
-        for e in (1, 2, 3) if l == 0 else ():
+        for e in (1, 2) if l == 0 else ():
             left(a_recv.at[l, e], base + 2 * e)
             left(p1_recv.at[l, e - 1], base + 2 * e + 1)
         left(n_recv.at[l], base + 8)

time: 109 us -> 102 us (0.936)
  Pallas kernels: 108 us -> 101 us
    pallas_call x1, Pallas kernels: 101 us -> 93.6 us  [decode(): pl.pallas_call(body, out_shape=(jax.ShapeDtypeStruct((2, SEQS, D), BF16),...]
where the time goes in v5:
time: 102 us
  Pallas kernels  101 us (99%)
    pallas_call x1, Pallas kernels, decode(): pl.pallas_call(body, out_shape=(jax.ShapeDtypeStruct((2, SEQS, D), BF16),...  93.6 us
    pallas_call x1, Pallas kernels, write_caches(): pl.pallas_call(write_body, out_shape=(jax.ShapeDtypeStruct(k.shape, BF16)...  7.01 us

profile of v5, /device:TPU:0, one launch (start us, length us, event | category | flops | bytes accessed | tf_op | source)
XLA Modules:
  0.0 101.9 jit_solution(13522052689874282759)
XLA Ops:
  0.6 0.0 copy-start
  0.6 0.0 copy-start.1
  0.7 0.0 copy-start.2
  0.7 93.6 %shard_map.220 = (bf16[2,2,1024]{2,1,0:T(2,128)(2,1)S(1)}, f32[16,1024]{1,0:T(8,128)S(1)}) custom-call(bf16[2,1024]{1,0:T(2,128)(2,1)} %h0_ref.1, bf16[2,1024]{1,0:T(2,128)(2,1)} %h1_ref.1, s32[2]{0:T(128)} %pos_ref.3, s32[2]{0:T(128)} %len_ref.1, f32[16,32]{1,0:T(8,128)} %bitcast.29, bf16[2,1024]{1,0:T(2,128)(2,1)} %gs_ref.1, bf16[2,1024]{1,0:T(2,128)(2,1)} %gc_ref.1, ...), custom_call_target="tpu_custom_call" | custom-call | flops 400000000 | bytes 33554432 | tf_op jit(solution)/shard_map/pallas_call | solution.py:466
  94.3 0.0 copy-done
  94.3 0.0 copy-done.1
  94.3 0.0 copy-done.2
  94.3 7.0 %shard_map.221 = (bf16[2,2,1024,1024]{3,2,1,0:T(8,128)(2,1)}, bf16[2,2,1024,1024]{3,2,1,0:T(8,128)(2,1)}) custom-call(s32[2]{0:T(128)S(1)} %copy-done.2, f32[16,1024]{1,0:T(8,128)S(1)} %get-tuple-element.8.new_ref, bf16[2,2,1024,1024]{3,2,1,0:T(8,128)(2,1)S(1)} %bitcast.22, bf16[2,2,1024,1024]{3,2,1,0:T(8,128)(2,1)S(1)} %bitcast.24), custom_call_target="tpu_custom_call" | custom-call | flops 1000000 | bytes 33554432 | tf_op jit(solution)/shard_map/pallas_call | solution.py:449
  101.3 0.6 copy.25
Async XLA Ops:
  0.6 93.6 %copy-start = (bf16[2,2,1024,16,64]{2,4,3,1,0:T(8,128)(2,1)S(1)}, bf16[2,2,1024,16,64]{2,4,3,1,0:T(8,128)(2,1)}, u32[]{:S(2)}) copy-start(bf16[2,2,1024,16,64]{2,4,3,1,0:T(8,128)(2,1)} %param.38) | copy-start | bytes 25165828
  0.6 93.6 %copy-start.1 = (bf16[2,2,1024,16,64]{2,4,3,1,0:T(8,128)(2,1)S(1)}, bf16[2,2,1024,16,64]{2,4,3,1,0:T(8,128)(2,1)}, u32[]{:S(2)}) copy-start(bf16[2,2,1024,16,64]{2,4,3,1,0:T(8,128)(2,1)} %param.39) | copy-start | bytes 25165828
  0.7 93.6 %copy-start.2 = (s32[2]{0:T(128)S(1)}, s32[2]{0:T(128)}, u32[]{:S(2)}) copy-start(s32[2]{0:T(128)} %pos_ref.3) | copy-start | bytes 28

commit v6 on v5

v6 whole, which is shorter than its diff:
```python
import functools

import jax
import jax.numpy as jnp
from jax import lax
from jax.experimental import pallas as pl
from jax.experimental.pallas import tpu as pltpu
from jax.sharding import PartitionSpec as P

NORM_EPS = 1e-6
BUCKET_EDGES = (16, 19, 21, 24, 27, 31, 35, 40, 46, 52, 59, 67, 77, 87, 99, 113)
BUCKET_STARTS = tuple(range(16)) + BUCKET_EDGES
F32 = jnp.float32
BF16 = jnp.bfloat16
LAYERS = 2
SEQS = 2
TOK = 2
BLK = 256
COLS = 4
ROWS = 4
PEERS = 16
D = 1024
HEADS = 16
T = 1024
E = 512
FB = 704
FS = 176
REPS = 4
PHASES = 4
BESIDE, ACROSS, TWIN, OWN = range(6, 10)
NEG = float("-inf")

SCHEDULE = {
    'n0': 'z01,y00,g00',
    'p0': 'y01,z02,g01',
    'o0': 'y02,z03,g02,z11',
    'r0': 'y03,y11,z12,g03',
    'c0': 'x0,y12,z13,y10,z21',
    'q0': 'y13,y21,z22,y20',
    'k0': 'e0,x1,y22,z23,z31',
    'm0': 'y23,y31,z32,y30',
    'u0': 'x2,y32,z33',
    'd0': 'e1,y33,g10',
    'n1': 'x3,e2,g11',
    'p1': 'e3,g12,g13',
}


def nt_dot(a, b):
    return lax.dot_general(a, b, (((1,), (1,)), ((), ())), preferred_element_type=F32)


def nn_dot(a, b):
    return jnp.dot(a, b, preferred_element_type=F32)


def body(h0_ref, h1_ref, pos_ref, len_ref, bias_ref, gs_ref, gc_ref, gm_ref,
         wq_hbm, wk_hbm, wv_hbm, wo_hbm, wcq_hbm, wco_hbm, wg_hbm, wu_hbm, wd_hbm,
         sk_hbm, sv_hbm, ck_hbm, cv_hbm,
         hid_ref, new_ref,
         sk, sv, ck, cv, self_bias, proj_w, gate_w, up_w, down_w,
         a_send, a_recv, p3_send, p3_recv, p1_send, p1_recv,
         n_send, n_recv, u_send, u_recv,
         rep, rep_send, rep_recv, cache_sem, weight_sem, mlp_send_sem, mlp_recv_sem, u_send_sem, u_recv_sem, send_sem, recv_sem):
    col = lax.axis_index('col')
    row = lax.axis_index('row')
    me = col * ROWS + row
    dp = lax.axis_index('dp')

    def peer_of(k):
        other = lax.rem(me + k, PEERS)
        return other, other // ROWS, lax.rem(other, ROWS)

    weight_copies = []
    for i, src in enumerate((wq_hbm, wk_hbm, wv_hbm, wo_hbm, wcq_hbm, wco_hbm)):
        cp = pltpu.make_async_copy(src, proj_w.at[i], weight_sem.at[i])
        cp.start()
        weight_copies.append(cp)
    cp = pltpu.make_async_copy(wd_hbm, down_w, weight_sem.at[6])
    cp.start()
    weight_copies.append(cp)
    cache_copies = []
    for l in range(LAYERS):
        for i, (src, dst) in enumerate(((sk_hbm, sk), (sv_hbm, sv), (ck_hbm, ck), (cv_hbm, cv))):
            cp = pltpu.make_async_copy(src.at[l], dst.at[l], cache_sem.at[l, i])
            cp.start()
            cache_copies.append(cp)

    barrier = pltpu.get_barrier_semaphore()
    for k in range(1, PEERS):
        _, c, r = peer_of(k)
        pl.semaphore_signal(barrier, inc=1, device_id={'col': c, 'row': r}, device_id_type=pl.DeviceIdType.MESH)
    pl.semaphore_signal(barrier, inc=1, device_id={'dp': 1 - dp}, device_id_type=pl.DeviceIdType.MESH)
    pl.semaphore_wait(barrier, PEERS)

    def exchange(send, recv, idx, by_row):
        def pick(r, other):
            return 0 if by_row is None else (r if by_row else other)

        for k in range(1, PEERS):
            other, c, r = peer_of(k)
            pltpu.make_async_remote_copy(
                src_ref=send.at[pick(r, other)], dst_ref=recv.at[me],
                send_sem=send_sem.at[idx], recv_sem=recv_sem.at[idx],
                device_id={'col': c, 'row': r}, device_id_type=pl.DeviceIdType.MESH).start()
        recv[me] = send[pick(row, me)]

    def arrive(recv, idx):
        part = recv.at[pl.ds(0, PEERS - 1)]
        pltpu.make_async_copy(part, part, recv_sem.at[idx]).wait()

    def left(recv, idx):
        part = recv.at[pl.ds(0, PEERS - 1)]
        pltpu.make_async_copy(part, part, send_sem.at[idx]).wait()

    def build_bias():
        jpos = lax.broadcasted_iota(jnp.int32, (HEADS, T), 1)
        for b in range(SEQS):
            p = pos_ref[b]
            for t in range(2):
                dist = p + t - jpos
                val = jnp.broadcast_to(bias_ref[:, 0:1], (HEADS, T))
                for n in range(1, 32):
                    val = jnp.where(dist >= BUCKET_STARTS[n], bias_ref[:, n:n + 1], val)
                self_bias[b, pl.ds(t * HEADS, HEADS), :] = jnp.where(jpos < p, val, NEG)

    r32 = lax.broadcasted_iota(jnp.int32, (32, 8), 0)
    c8 = lax.broadcasted_iota(jnp.int32, (32, 8), 1)
    db0 = jnp.concatenate([bias_ref[:, 0:1]] * 2, axis=0)
    db1 = jnp.concatenate([bias_ref[:, 1:2]] * 2, axis=0)
    new_bias = jnp.where(c8 == 0, jnp.where(r32 < HEADS, db0, db1),
                         jnp.where((c8 == 1) & (r32 >= HEADS), db0, NEG))
    head_of = (lax.broadcasted_iota(jnp.int32, (32, D), 1) // 64) == lax.rem(
        lax.broadcasted_iota(jnp.int32, (32, D), 0), HEADS)
    jcross = lax.broadcasted_iota(jnp.int32, (32, E), 1)

    def rms(x, gain):
        mean_sq = jnp.mean(x * x, axis=-1, keepdims=True)
        return x * lax.rsqrt(mean_sq + NORM_EPS) * gain.astype(F32)

    def column(vec, r):
        return vec[:, r * BLK:(r + 1) * BLK]

    def rows_of(prod, s):
        return prod[s * TOK:(s + 1) * TOK]

    def put_act(vec, buf):
        for r in range(ROWS):
            buf[r] = column(vec, r)

    def gather_act(recv):
        rows = jnp.concatenate([recv[s].astype(F32) for s in range(PEERS)], axis=0)
        return rows.astype(BF16)

    def spread_query(q):
        both = jnp.concatenate([jnp.broadcast_to(q[t:t + 1, :], (HEADS, D)) for t in range(TOK)], axis=0)
        return jnp.where(head_of, both, 0.0).astype(BF16)

    def fold_heads(mixed):
        keep = jnp.where(head_of, mixed, 0.0)
        return jnp.concatenate([jnp.sum(keep[:HEADS], axis=0, keepdims=True),
                                jnp.sum(keep[HEADS:], axis=0, keepdims=True)], axis=0)

    def row_sum(get):
        return [(get(c * ROWS) + get(c * ROWS + 1)) + (get(c * ROWS + 2) + get(c * ROWS + 3)) for c in range(COLS)]

    def round_bf16(v):
        return v.astype(BF16).astype(F32)

    def project(vec, which, b, l, e, names):
        idx = sem_of(b, l, e)
        put_act(vec, a_send.at[b, l, e])
        exchange(a_send.at[b, l, e], a_recv.at[b, l, e], idx, True)
        yield names[0]
        arrive(a_recv.at[b, l, e], idx)
        prod = nn_dot(gather_act(a_recv.at[b, l, e]), proj_w[which, l])
        yield from back(prod, b, l, e, names[1])
        return back_sum(b, l, e)

    def sem_of(b, l, e):
        return ((b * LAYERS) + l) * 2 * PHASES + 2 * e

    def back(prod, b, l, e, name):
        for s in range(PEERS):
            p1_send[b, l, e, s] = rows_of(prod, s)
        exchange(p1_send.at[b, l, e], p1_recv.at[b, l, e], sem_of(b, l, e) + 1, False)
        yield name
        arrive(p1_recv.at[b, l, e], sem_of(b, l, e) + 1)

    def back_sum(b, l, e):
        return round_bf16(jnp.concatenate(row_sum(lambda s: p1_recv[b, l, e, s]), axis=1))

    def mlp_in(l, share):
        i = share // 2
        src, dst = ((wg_hbm, gate_w), (wu_hbm, up_w))[i]
        for k in range(share % 2, ROWS, 2):
            r = lax.rem(row + k, ROWS)
            part = src.at[l, pl.ds(pl.multiple_of(r * FS, HEADS), FS), :]
            if k == 0:
                pltpu.make_async_copy(part, dst.at[l, row], mlp_recv_sem.at[l, i]).start()
            else:
                pltpu.make_async_remote_copy(
                    src_ref=part, dst_ref=dst.at[l, row], send_sem=mlp_send_sem.at[l, i],
                    recv_sem=mlp_recv_sem.at[l, i], device_id={'col': col, 'row': r},
                    device_id_type=pl.DeviceIdType.MESH).start()

    def send_u(b, l):
        src, dst = u_send.at[b, l], u_recv.at[b, l, row]

        def away(c):
            pltpu.make_async_remote_copy(
                src_ref=src, dst_ref=dst, send_sem=u_send_sem.at[b, l], recv_sem=u_recv_sem.at[b, l],
                device_id={'col': c, 'row': col}, device_id_type=pl.DeviceIdType.MESH).start()

        for k in range(1, COLS):
            away(lax.rem(col + k, COLS))

        @pl.when(col != row)
        def _():
            away(col)

        @pl.when(col == row)
        def _():
            pltpu.make_async_copy(src, dst, u_recv_sem.at[b, l]).start()

    own = (wco_hbm.at[0], wo_hbm.at[1], wcq_hbm.at[1], wco_hbm.at[1])
    flip = lax.rem(row + 2, ROWS)
    twin = row + 1 - 2 * lax.rem(row, 2)
    first_row = pl.multiple_of(dp * 128, 128)

    def half(m, j):
        return rep.at[m, j, pl.ds(first_row, 128), :]

    def pass_on(m, step, src, dst, device):
        pltpu.make_async_remote_copy(
            src_ref=src, dst_ref=dst, send_sem=rep_send.at[m], recv_sem=rep_recv.at[m, step],
            device_id=device, device_id_type=pl.DeviceIdType.MESH).start()

    def took(m, step, blocks):
        part = rep.at[m, pl.ds(0, blocks)]
        pltpu.make_async_copy(part, part, rep_recv.at[m, step]).wait()

    def took_halves(m, step, halves):
        part = rep.at[m, pl.ds(0, halves), pl.ds(0, 128), :]
        pltpu.make_async_copy(part, part, rep_recv.at[m, step]).wait()

    def own_half(m):
        return own[m].at[pl.ds(first_row, 128), :]

    def rep_z(m, t):
        if t == 1:
            pltpu.make_async_copy(own[m], rep.at[m, me], rep_recv.at[m, OWN]).start()
        for way, (there, plane, onward) in enumerate((
                ((col >= t - 1) & (col < COLS - 1), col - (t - 1), col + 1),
                ((col + t <= COLS) & (col > 0), col + (t - 1), col - 1))):
            @pl.when(there)
            def _():
                j = plane * ROWS + row
                src = own_half(m) if t == 1 else half(m, j)
                pass_on(m, way * 3 + t - 1, src, half(m, j), {'col': onward})

    def rep_y(m, t):
        if t == 0:
            pass_on(m, BESIDE, own_half(m), half(m, me), {'row': flip})
            return
        for way, (there, plane) in enumerate(((col >= t, col - t), (col + t < COLS, col + t))):
            @pl.when(there)
            def _():
                j = plane * ROWS + row
                took_halves(m, way * 3 + t - 1, 1)
                pass_on(m, BESIDE, half(m, j), half(m, j), {'row': flip})
                pass_on(m, ACROSS, half(m, j), half(m, j), {'dp': 1 - dp})

    def rep_x(m):
        took_halves(m, BESIDE, COLS)
        for c in range(COLS):
            j = c * ROWS + flip
            pass_on(m, ACROSS, half(m, j), half(m, j), {'dp': 1 - dp})

    def rep_e(m):
        took_halves(m, ACROSS, 2 * COLS - 1)
        took(m, OWN, 1)
        for c in range(COLS):
            for r in (row, flip):
                j = c * ROWS + r
                pass_on(m, TWIN, rep.at[m, j], rep.at[m, j], {'row': twin})

    def rep_left(m):
        def gone(part):
            pltpu.make_async_copy(part, part, rep_send.at[m]).wait()

        gone(rep.at[m, pl.ds(0, 2 * COLS)])
        gone(rep.at[m, pl.ds(0, 3 * COLS - 1), pl.ds(0, 128), :])
        for t in range(1, COLS):
            for there in ((col >= t - 1) & (col < COLS - 1), (col + t <= COLS) & (col > 0)):
                @pl.when(there)
                def _():
                    gone(rep.at[m, 0, pl.ds(0, 128), :])

    def add_up(terms):
        return functools.reduce(jnp.add, terms)

    def local_project(vec, m, b):
        if b == 0:
            took(m, TWIN, 2 * COLS)
        sums = []
        for c in range(COLS):
            sums.append(add_up([nn_dot(column(vec, r), rep[m, c * ROWS + r]) for r in range(ROWS)]))
        return round_bf16(jnp.concatenate(sums, axis=1))

    def fill(name):
        for item in SCHEDULE.get(name, '').split(','):
            if item:
                move = {'g': mlp_in, 'z': rep_z, 'y': rep_y, 'x': rep_x, 'e': rep_e}[item[0]]
                move(*[int(digit) for digit in item[1:]])

    def mlp_arrive(l):
        for i, dst in enumerate((gate_w, up_w)):
            pltpu.make_async_copy(dst.at[l], dst.at[l], mlp_recv_sem.at[l, i]).wait()

    def mlp_left(l):
        for i, dst in enumerate((gate_w, up_w)):
            part = dst.at[l, pl.ds(0, ROWS - 1)]
            pltpu.make_async_copy(part, part, mlp_send_sem.at[l, i]).wait()
        for b in range(SEQS):
            part = u_recv.at[b, l, pl.ds(0, COLS - 1)]
            pltpu.make_async_copy(part, part, u_send_sem.at[b, l]).wait()

            @pl.when(col != row)
            def _():
                one = u_recv.at[b, l, 0]
                pltpu.make_async_copy(one, one, u_send_sem.at[b, l]).wait()

    whole = {'o0': None, 'c0': None, 'k0': 0, 'o1': 1, 'c1': 2, 'k1': 3}

    def apply(vec, which, b, l, e, names):
        m = whole[names[0]]
        if m is None:
            return (yield from project(vec, which, b, l, e, names))
        return local_project(vec, m, b)

    def self_attention(q, k, v, b, l):
        qb = spread_query(q)
        zeros = jnp.zeros((8 - TOK, D), F32)
        kn = jnp.concatenate([k, zeros], axis=0).astype(BF16)
        vn = jnp.concatenate([v, zeros], axis=0).astype(BF16)
        old = nn_dot(qb, sk[l, b]) + self_bias[b]
        new = nt_dot(qb, kn) + new_bias
        top = jnp.maximum(jnp.max(old, axis=1, keepdims=True), jnp.max(new, axis=1, keepdims=True))
        e_old = jnp.exp(old - top)
        e_new = jnp.exp(new - top)
        total = jnp.sum(e_old, axis=1, keepdims=True) + jnp.sum(e_new, axis=1, keepdims=True)
        mixed = nt_dot((e_old / total).astype(BF16), sv[l, b]) + nn_dot((e_new / total).astype(BF16), vn)
        return fold_heads(mixed).astype(BF16)

    def cross_attention(q, b, l):
        sc = jnp.where(jcross < len_ref[b], nn_dot(spread_query(q), ck[l, b]), NEG)
        ex = jnp.exp(sc - jnp.max(sc, axis=1, keepdims=True))
        probs = (ex / jnp.sum(ex, axis=1, keepdims=True)).astype(BF16)
        return fold_heads(nt_dot(probs, cv[l, b])).astype(BF16)

    def stream(b, done):
        x = jnp.concatenate([h[b:b + 1].astype(F32) for h in (h0_ref, h1_ref)], axis=0)
        for l in range(LAYERS):
            idx = sem_of(b, l, 0)
            put_act(rms(x, gs_ref[l:l + 1, :]).astype(BF16), a_send.at[b, l, 0])
            exchange(a_send.at[b, l, 0], a_recv.at[b, l, 0], idx, True)
            yield f'n{l}'
            arrive(a_recv.at[b, l, 0], idx)
            act = gather_act(a_recv.at[b, l, 0])
            for i in range(3):
                prod = nn_dot(act, proj_w[i, l])
                for s in range(PEERS):
                    p3_send[b, l, s, :, i * BLK:(i + 1) * BLK] = rows_of(prod, s)
            exchange(p3_send.at[b, l], p3_recv.at[b, l], idx + 1, False)
            yield f'p{l}'
            arrive(p3_recv.at[b, l], idx + 1)
            sums = row_sum(lambda s: p3_recv[b, l, s])
            q, k, v = (round_bf16(jnp.concatenate([column(sm, i) for sm in sums], axis=1)) for i in range(3))
            for kv, fresh in enumerate((k, v)):
                new_ref[pl.ds(((l * 2 + kv) * SEQS + b) * TOK, TOK), :] = fresh
            if b == 0:
                cache_copies[l * 4].wait()
                cache_copies[l * 4 + 1].wait()
            x = x + (yield from apply(self_attention(q, k, v, b, l), 3, b, l, 1, (f'o{l}', f'r{l}')))

            n = rms(x, gc_ref[l:l + 1, :]).astype(BF16)
            q = yield from apply(n, 4, b, l, 2, (f'c{l}', f'q{l}'))
            if b == 0:
                fill(f'k{l}')
                cache_copies[l * 4 + 2].wait()
                cache_copies[l * 4 + 3].wait()
            x = x + (yield from apply(cross_attention(q, b, l), 5, b, l, 3, (f'k{l}', '')))

            n_send[b, l, 0] = rms(x, gm_ref[l:l + 1, :]).astype(BF16)
            idx = sem_of(b, l, 3)
            exchange(n_send.at[b, l], n_recv.at[b, l], idx, None)
            yield f'm{l}'
            if b == 0:
                mlp_arrive(l)
            arrive(n_recv.at[b, l], idx)
            act = gather_act(n_recv.at[b, l])
            gate, up = (add_up([nt_dot(column(act, r), w[l, r]) for r in range(ROWS)]) for w in (gate_w, up_w))
            u_send[b, l] = (jax.nn.silu(round_bf16(gate)) * round_bf16(up)).astype(BF16)
            send_u(b, l)
            yield f'u{l}'
            pltpu.make_async_copy(u_recv.at[b, l], u_recv.at[b, l], u_recv_sem.at[b, l]).wait()
            prod = add_up([nn_dot(u_recv[b, l, r], down_w[l, r * FS:(r + 1) * FS]) for r in range(ROWS)])
            yield from back(prod, b, l, 3, f'd{l}')
            x = x + back_sum(b, l, 3)
        done.append(x)

    done = []
    streams = [stream(b, done) for b in range(SEQS)]
    while True:
        names = [next(streams[0], '')]
        if not names[0]:
            next(streams[1], '')
            break
        fill(names[0])
        next(streams[1], '')
        if names[0] == 'n0':
            build_bias()
            for cp in weight_copies:
                cp.wait()
    for t in range(TOK):
        hid_ref[t] = jnp.concatenate([x[t:t + 1] for x in done], axis=0).astype(BF16)
    for l in range(LAYERS):
        for b in range(SEQS):
            left(a_recv.at[b, l, 0], sem_of(b, l, 0))
            left(p3_recv.at[b, l], sem_of(b, l, 0) + 1)
            for e in range(1, 3 - 2 * l):
                left(a_recv.at[b, l, e], sem_of(b, l, e))
                left(p1_recv.at[b, l, e], sem_of(b, l, e) + 1)
            left(n_recv.at[b, l], sem_of(b, l, 3))
            left(p1_recv.at[b, l, 3], sem_of(b, l, 3) + 1)
        mlp_left(l)
    for m in range(REPS):
        rep_left(m)


def write_body(pos_ref, new_ref, k_ref, v_ref, ko_ref, vo_ref, cols, patch, sem):
    lanes = lax.broadcasted_iota(jnp.int32, (D, 128), 1)
    blocks = [(l, b, kv) for l in range(LAYERS) for b in range(SEQS) for kv in range(2)]

    def refs(kv):
        return (k_ref, ko_ref) if kv == 0 else (v_ref, vo_ref)

    def tiles(l, b, kv, put):
        first, second = pos_ref[b] // 128, (pos_ref[b] + 1) // 128
        src, dst = refs(kv)
        for i in range(T // 128):
            out = dst.at[l, b, :, pl.ds(i * 128, 128)]
            put(i, first, second, src.at[l, b, :, pl.ds(i * 128, 128)], out)

    for l, b, kv in blocks:
        def plain(i, first, second, src, out):
            @pl.when((first != i) & (second != i))
            def _():
                pltpu.make_async_copy(src, out, sem.at[l, b, kv]).start()

        tiles(l, b, kv, plain)

    cols[...] = jnp.transpose(new_ref[...])
    for l, b, kv in blocks:
        p = pos_ref[b]
        at = ((l * 2 + kv) * SEQS + b) * TOK
        src, _ = refs(kv)
        for q in range(2):
            start = pl.multiple_of(((p + q) // 128) * 128, 128)
            old = src[l, b, :, pl.ds(start, 128)].astype(F32)
            fresh = jnp.where(lanes + start == p, cols[:, at:at + 1],
                              jnp.where(lanes + start == p + 1, cols[:, at + 1:at + 2], old))
            patch[l, b, kv, q] = fresh.astype(BF16)

        def changed(i, first, second, src, out):
            @pl.when(first == i)
            def _():
                pltpu.make_async_copy(patch.at[l, b, kv, 0], out, sem.at[l, b, kv]).start()

            @pl.when((second == i) & (first != i))
            def _():
                pltpu.make_async_copy(patch.at[l, b, kv, 1], out, sem.at[l, b, kv]).start()

        tiles(l, b, kv, changed)
    for l, b, kv in blocks:
        src, dst = refs(kv)
        pltpu.make_async_copy(src.at[l, b], dst.at[l, b], sem.at[l, b, kv]).wait()


def write_caches(pos, new, k, v):
    vmem = pl.BlockSpec(memory_space=pltpu.VMEM)
    return pl.pallas_call(
        write_body,
        out_shape=(jax.ShapeDtypeStruct(k.shape, BF16),) * 2,
        in_specs=[pl.BlockSpec(memory_space=pltpu.SMEM), vmem, vmem, vmem],
        out_specs=(pl.BlockSpec(memory_space=pltpu.HBM),) * 2,
        scratch_shapes=[pltpu.VMEM((D, 16), F32), pltpu.VMEM((LAYERS, SEQS, 2, 2, D, 128), BF16),
                        pltpu.SemaphoreType.DMA((LAYERS, SEQS, 2))],
        compiler_params=pltpu.CompilerParams(vmem_limit_bytes=28 * 1024 * 1024),
        cost_estimate=pl.CostEstimate(flops=1000000, bytes_accessed=32 << 20, transcendentals=0),
    )(pos, new, k, v)


def decode(*args):
    both = (SEQS, LAYERS)
    vmem = pl.BlockSpec(memory_space=pltpu.VMEM)
    smem = pl.BlockSpec(memory_space=pltpu.SMEM)
    hbm = pl.BlockSpec(memory_space=pltpu.HBM)
    args = tuple(pltpu.with_memory_space_constraint(a, pltpu.HBM) for a in args)
    return pl.pallas_call(
        body,
        out_shape=(jax.ShapeDtypeStruct((2, SEQS, D), BF16),
                   jax.ShapeDtypeStruct((16, D), F32)),
        in_specs=[vmem, vmem, smem, smem] + [vmem] * 4 + [hbm] * 13,
        out_specs=(vmem,) * 2,
        scratch_shapes=[
            pltpu.VMEM((LAYERS, SEQS, D, T), BF16),
            pltpu.VMEM((LAYERS, SEQS, D, T), BF16),
            pltpu.VMEM((LAYERS, SEQS, D, E), BF16),
            pltpu.VMEM((LAYERS, SEQS, D, E), BF16),
            pltpu.VMEM((SEQS, 32, T), F32),
            pltpu.VMEM((6, LAYERS, 256, 256), BF16),
            pltpu.VMEM((LAYERS, ROWS, FS, 256), BF16),
            pltpu.VMEM((LAYERS, ROWS, FS, 256), BF16),
            pltpu.VMEM((LAYERS, FB, 256), BF16),
            pltpu.VMEM(both + (3, ROWS, TOK, BLK), BF16),
            pltpu.VMEM(both + (3, PEERS, TOK, BLK), BF16),
            pltpu.VMEM(both + (PEERS, TOK, 3 * BLK), F32),
            pltpu.VMEM(both + (PEERS, TOK, 3 * BLK), F32),
            pltpu.VMEM(both + (PHASES, PEERS, TOK, BLK), F32),
            pltpu.VMEM(both + (PHASES, PEERS, TOK, BLK), F32),
            pltpu.VMEM(both + (1, TOK, D), BF16),
            pltpu.VMEM(both + (PEERS, TOK, D), BF16),
            pltpu.VMEM(both + (PEERS * TOK, FS), BF16),
            pltpu.VMEM(both + (ROWS, PEERS * TOK, FS), BF16),
            pltpu.VMEM((REPS, PEERS, 256, 256), BF16),
            pltpu.SemaphoreType.DMA((REPS,)),
            pltpu.SemaphoreType.DMA((REPS, OWN + 1)),
            pltpu.SemaphoreType.DMA((LAYERS, 4)),
            pltpu.SemaphoreType.DMA((7,)),
            pltpu.SemaphoreType.DMA((LAYERS, 2)),
            pltpu.SemaphoreType.DMA((LAYERS, 2)),
            pltpu.SemaphoreType.DMA(both),
            pltpu.SemaphoreType.DMA(both),
            pltpu.SemaphoreType.DMA((SEQS * LAYERS * 2 * PHASES,)),
            pltpu.SemaphoreType.DMA((SEQS * LAYERS * 2 * PHASES,)),
        ],
        compiler_params=pltpu.CompilerParams(collective_id=0, has_side_effects=True,
                                             vmem_limit_bytes=44 * 1024 * 1024),
        cost_estimate=pl.CostEstimate(flops=400000000, bytes_accessed=32 << 20, transcendentals=0),
    )(*args)


def solution(mesh):
    batch_axes = ('dp', 'col', 'row')

    def local_step(h_first, h_second, start_pos, enc_lens, dec_bias, norm_self, norm_cross, norm_mlp,
                   w_query, w_key, w_value, w_out, w_cquery, w_cout, w_gate, w_up, w_down,
                   self_k, self_v, cross_k, cross_v):
        def flat(cache):
            l, b, t, h, d = cache.shape
            return cache.transpose(0, 1, 3, 4, 2).reshape(l, b, h * d, t)

        def unflat(cache):
            l, b, _, t = cache.shape
            return cache.reshape(l, b, HEADS, 64, t).transpose(0, 1, 4, 2, 3)

        keys, vals = flat(self_k), flat(self_v)
        hidden, new = decode(
            h_first, h_second, start_pos, enc_lens, dec_bias.T, norm_self, norm_cross, norm_mlp,
            w_query, w_key, w_value, w_out, w_cquery, w_cout,
            w_gate.transpose(0, 2, 1), w_up.transpose(0, 2, 1), w_down,
            keys, vals, flat(cross_k), flat(cross_v))
        keys, vals = write_caches(start_pos, new, keys, vals)
        return hidden, unflat(keys), unflat(vals)

    row_spec = P(batch_axes, None)
    seq_spec = P(batch_axes)
    weight_spec = P(None, 'row', 'col')
    cache_spec = P(None, batch_axes)
    in_specs = (row_spec, row_spec, seq_spec, seq_spec, P(), P(), P(), P()) + (weight_spec,) * 9 + (cache_spec,) * 4
    out_specs = (P(None, batch_axes), cache_spec, cache_spec)
    return jax.shard_map(local_step, mesh=mesh, in_specs=in_specs, out_specs=out_specs, check_vma=False)
```

time: 102 us -> 97.8 us (0.959)
  Pallas kernels: 101 us -> 96.3 us
    pallas_call x1, Pallas kernels: 93.6 us -> 89.3 us  [decode(): pl.pallas_call(body, out_shape=(jax.ShapeDtypeStruct((2, SEQS, D), BF16),...]
where the time goes in v6:
time: 97.8 us; the launch traced here: 97.6 us
  Pallas kernels  96.3 us (98%)
    pallas_call x1, Pallas kernels, decode(): pl.pallas_call(body, out_shape=(jax.ShapeDtypeStruct((2, SEQS, D), BF16),...  89.3 us
    pallas_call x1, Pallas kernels, write_caches(): pl.pallas_call(write_body, out_shape=(jax.ShapeDtypeStruct(k.shape, BF16)...  7.01 us

profile of v6, /device:TPU:0, one launch (start us, length us, event | category | flops | bytes accessed | tf_op | source)
XLA Modules:
  0.0 97.6 jit_solution(12355158037029655265)
XLA Ops:
  0.6 0.0 copy-start
  0.6 0.0 copy-start.1
  0.7 0.0 copy-start.2
  0.7 89.3 %shard_map.220 = (bf16[2,2,1024]{2,1,0:T(2,128)(2,1)S(1)}, f32[16,1024]{1,0:T(8,128)S(1)}) custom-call(bf16[2,1024]{1,0:T(2,128)(2,1)} %h0_ref.1, bf16[2,1024]{1,0:T(2,128)(2,1)} %h1_ref.1, s32[2]{0:T(128)} %pos_ref.3, s32[2]{0:T(128)} %len_ref.1, f32[16,32]{1,0:T(8,128)} %bitcast.29, bf16[2,1024]{1,0:T(2,128)(2,1)} %gs_ref.1, bf16[2,1024]{1,0:T(2,128)(2,1)} %gc_ref.1, ...), custom_call_target="tpu_custom_call" | custom-call | flops 400000000 | bytes 33554432 | tf_op jit(solution)/shard_map/pallas_call | solution.py:511
  89.9 0.0 copy-done
  89.9 0.0 copy-done.1
  90.0 0.0 copy-done.2
  90.0 7.0 %shard_map.221 = (bf16[2,2,1024,1024]{3,2,1,0:T(8,128)(2,1)}, bf16[2,2,1024,1024]{3,2,1,0:T(8,128)(2,1)}) custom-call(s32[2]{0:T(128)S(1)} %copy-done.2, f32[16,1024]{1,0:T(8,128)S(1)} %get-tuple-element.8.new_ref, bf16[2,2,1024,1024]{3,2,1,0:T(8,128)(2,1)S(1)} %bitcast.22, bf16[2,2,1024,1024]{3,2,1,0:T(8,128)(2,1)S(1)} %bitcast.24), custom_call_target="tpu_custom_call" | custom-call | flops 1000000 | bytes 33554432 | tf_op jit(solution)/shard_map/pallas_call | solution.py:493
  97.0 0.6 copy.25
Async XLA Ops:
  0.6 89.3 %copy-start = (bf16[2,2,1024,16,64]{2,4,3,1,0:T(8,128)(2,1)S(1)}, bf16[2,2,1024,16,64]{2,4,3,1,0:T(8,128)(2,1)}, u32[]{:S(2)}) copy-start(bf16[2,2,1024,16,64]{2,4,3,1,0:T(8,128)(2,1)} %param.38) | copy-start | bytes 25165828
  0.6 89.3 %copy-start.1 = (bf16[2,2,1024,16,64]{2,4,3,1,0:T(8,128)(2,1)S(1)}, bf16[2,2,1024,16,64]{2,4,3,1,0:T(8,128)(2,1)}, u32[]{:S(2)}) copy-start(bf16[2,2,1024,16,64]{2,4,3,1,0:T(8,128)(2,1)} %param.39) | copy-start | bytes 25165828
  0.7 89.3 %copy-start.2 = (s32[2]{0:T(128)S(1)}, s32[2]{0:T(128)}, u32[]{:S(2)}) copy-start(s32[2]{0:T(128)} %pos_ref.3) | copy-start | bytes 28

commit v7 on v6

--- a/solution.py
+++ b/solution.py
@@ -97,7 +97,7 @@
         def pick(r, other):
             return 0 if by_row is None else (r if by_row else other)
 
-        for k in range(1, PEERS):
+        for k in sorted(range(1, PEERS), key=lambda k: abs(2 * k - PEERS)):
             other, c, r = peer_of(k)
             pltpu.make_async_remote_copy(
                 src_ref=send.at[pick(r, other)], dst_ref=recv.at[me],
@@ -417,8 +417,12 @@
         if not names[0]:
             next(streams[1], '')
             break
-        fill(names[0])
+        late = names[0][0] in 'npm'
+        if not late:
+            fill(names[0])
         next(streams[1], '')
+        if late:
+            fill(names[0])
         if names[0] == 'n0':
             build_bias()
             for cp in weight_copies:

time: 97.8 us -> 97 us (level)
  no operation moved by 1% of the time
where the time goes in v7:
time: 97 us; the launch traced here: 96.8 us
  Pallas kernels  95.5 us (98%)
    pallas_call x1, Pallas kernels, decode(): pl.pallas_call(body, out_shape=(jax.ShapeDtypeStruct((2, SEQS, D), BF16),...  88.5 us
    pallas_call x1, Pallas kernels, write_caches(): pl.pallas_call(write_body, out_shape=(jax.ShapeDtypeStruct(k.shape, BF16)...  7.01 us

profile of v7, /device:TPU:0, one launch (start us, length us, event | category | flops | bytes accessed | tf_op | source)
XLA Modules:
  0.0 96.8 jit_solution(5170104069057291231)
XLA Ops:
  0.6 0.0 copy-start
  0.6 0.0 copy-start.1
  0.7 0.0 copy-start.2
  0.7 88.5 %shard_map.220 = (bf16[2,2,1024]{2,1,0:T(2,128)(2,1)S(1)}, f32[16,1024]{1,0:T(8,128)S(1)}) custom-call(bf16[2,1024]{1,0:T(2,128)(2,1)} %h0_ref.1, bf16[2,1024]{1,0:T(2,128)(2,1)} %h1_ref.1, s32[2]{0:T(128)} %pos_ref.3, s32[2]{0:T(128)} %len_ref.1, f32[16,32]{1,0:T(8,128)} %bitcast.29, bf16[2,1024]{1,0:T(2,128)(2,1)} %gs_ref.1, bf16[2,1024]{1,0:T(2,128)(2,1)} %gc_ref.1, ...), custom_call_target="tpu_custom_call" | custom-call | flops 400000000 | bytes 33554432 | tf_op jit(solution)/shard_map/pallas_call | solution.py:515
  89.2 0.0 copy-done
  89.2 0.0 copy-done.1
  89.2 0.0 copy-done.2
  89.2 7.0 %shard_map.221 = (bf16[2,2,1024,1024]{3,2,1,0:T(8,128)(2,1)}, bf16[2,2,1024,1024]{3,2,1,0:T(8,128)(2,1)}) custom-call(s32[2]{0:T(128)S(1)} %copy-done.2, f32[16,1024]{1,0:T(8,128)S(1)} %get-tuple-element.8.new_ref, bf16[2,2,1024,1024]{3,2,1,0:T(8,128)(2,1)S(1)} %bitcast.22, bf16[2,2,1024,1024]{3,2,1,0:T(8,128)(2,1)S(1)} %bitcast.24), custom_call_target="tpu_custom_call" | custom-call | flops 1000000 | bytes 33554432 | tf_op jit(solution)/shard_map/pallas_call | solution.py:497
  96.2 0.6 copy.25
Async XLA Ops:
  0.6 88.5 %copy-start = (bf16[2,2,1024,16,64]{2,4,3,1,0:T(8,128)(2,1)S(1)}, bf16[2,2,1024,16,64]{2,4,3,1,0:T(8,128)(2,1)}, u32[]{:S(2)}) copy-start(bf16[2,2,1024,16,64]{2,4,3,1,0:T(8,128)(2,1)} %param.38) | copy-start | bytes 25165828
  0.6 88.5 %copy-start.1 = (bf16[2,2,1024,16,64]{2,4,3,1,0:T(8,128)(2,1)S(1)}, bf16[2,2,1024,16,64]{2,4,3,1,0:T(8,128)(2,1)}, u32[]{:S(2)}) copy-start(bf16[2,2,1024,16,64]{2,4,3,1,0:T(8,128)(2,1)} %param.39) | copy-start | bytes 25165828
  0.7 88.5 %copy-start.2 = (s32[2]{0:T(128)S(1)}, s32[2]{0:T(128)}, u32[]{:S(2)}) copy-start(s32[2]{0:T(128)} %pos_ref.3) | copy-start | bytes 28
